TPU v7x, 512 devices: a whole 4x4x16 slice. The times are simulated.
512 devices in a mesh: cells: 128 (over z, x_hi, y), genes: 4 (over x_lo, core).
Axes of the slice: x: 4 (x_hi: 2, x_lo: 2; x = x_hi * 2 + x_lo), y: 4, z: 16, core: 2. Of those that a mesh axis runs over, the one named last changes fastest.
Arguments:
- counts: bfloat16 [16384, 16384], P('cells', 'genes'), may hold values from 0 to 254
- occupancy: int32 [128, 128], P('cells', 'genes'), may hold values 0 or 1
- start_basis: bfloat16 [64, 16384], P(None, 'genes'), may hold values from -0.046875 to 0.046875
Outputs:
- new_basis: float32 [64, 16384], P(None, ('genes', 'cells'))
All inputs are finite; a program needn't handle non-finite values. No bound on the sum of `occupancy` on one device may be relied on, other than what follows from the above.
Results may differ from a plain program's by a relative error of at most 0.01.
Values sent between devices are 32-bit elements; how exact they have to be, the bound alone decides.
A program may use at most 64 MiB of HBM per device.

v0:
```python
import math

import jax
import jax.numpy as jnp
from jax import lax
from jax.sharding import Mesh
from jax.sharding import PartitionSpec as P

CELLS = ("cells_0", "cells_1", "cells_2")
GENES_CELLS = ("genes", "cells_0", "cells_1", "cells_2")


def copy_for_each(shard, axis):
    copies = jnp.broadcast_to(shard, (lax.axis_size(axis), *shard.shape))
    return lax.all_to_all(copies, axis, split_axis=0, concat_axis=0, tiled=True)


def over_copies(shard, axis):
    return copy_for_each(shard, axis).sum(axis=0)


def one_axis_at_a_time(shard, axes):
    far, near = axes
    return over_copies(over_copies(shard, near), far)


def in_blocks(shard, dim, peers):
    before, after = (shard.shape[:dim], shard.shape[dim + 1 :])
    return jnp.moveaxis(shard.reshape(*before, peers, -1, *after), dim, 0)


def sent_and_summed(shard, axis, dim):
    peers = lax.axis_size(axis)
    blocks = lax.all_to_all(in_blocks(shard, dim, peers), axis, 0, 0, tiled=True)
    return jnp.sum(blocks, axis=0)


def sum_by_axis(shard, axes, dim):
    far, near = axes
    own = sent_and_summed(in_blocks(shard, dim, lax.axis_size(far)), near, dim + 1)
    return jnp.sum(lax.all_to_all(own, far, 0, 0, tiled=True), axis=0)


def padded_to(lines, peers):
    spare = -lines.shape[0] % peers
    if not spare:
        return lines
    return jnp.concatenate([lines, jnp.zeros((spare, *lines.shape[1:]), lines.dtype)])


def in_order(blocks, dim):
    dims = list(blocks.shape[1:])
    dims[dim] *= blocks.shape[0]
    return jnp.moveaxis(blocks, 0, dim).reshape(dims)


def whole_of(shard, axes, dim):
    far, near = axes
    first = copy_for_each(shard, far)
    blocks = jnp.swapaxes(copy_for_each(first, near), 0, 1)
    return in_order(blocks.reshape(-1, *shard.shape), dim)


def sum_by_parts(shard, axes):
    lines = shard.reshape(-1)
    own = sum_by_axis(padded_to(lines, lax.axis_size(axes[0]) * lax.axis_size(axes[1])), axes, 0)
    whole = whole_of(own, axes, 0)
    return whole[: len(lines)].reshape(shard.shape)


def on_device(counts, occupancy, start_basis):
    tile_rows, tile_cols = occupancy.shape
    cell_count, gene_count = counts.shape
    tile_edge = cell_count // tile_rows
    comp_count = start_basis.shape[0]
    logged = jnp.log1p(counts.astype(jnp.float32)).reshape(
        tile_rows, tile_edge, tile_cols, tile_edge
    )
    logged = (logged * occupancy.astype(jnp.float32)[:, None, :, None]).reshape(
        cell_count, gene_count
    )
    totals = one_axis_at_a_time(jnp.sum(logged, axis=0), (("cells_0", "cells_1"), "cells_2"))
    gene_mean = totals / (cell_count * lax.axis_size(CELLS))
    centered = (logged - gene_mean).astype(jnp.bfloat16)
    partial_value = lax.dot_general(
        start_basis, centered, (((1,), (1,)), ((), ())), preferred_element_type=jnp.float32
    )
    share_cols = gene_count // lax.axis_size(CELLS)
    scores = over_copies(partial_value, "genes")
    score_high = scores.astype(jnp.bfloat16)
    score_low = (scores - score_high.astype(jnp.float32)).astype(jnp.bfloat16)
    stacked = jnp.concatenate([score_high, score_low], axis=0)
    both = jnp.dot(stacked, centered, preferred_element_type=jnp.float32)
    product_term = both[:comp_count] + both[comp_count:]
    spread = sum_by_parts(product_term, (("cells_0", "cells_1"), "cells_2"))
    local_gram = lax.dot_general(
        spread,
        spread,
        (((1,), (1,)), ((), ())),
        precision=lax.Precision.HIGHEST,
        preferred_element_type=jnp.float32,
    )
    gram_sum = over_copies(local_gram, "genes")
    factor = jnp.linalg.cholesky(gram_sum)
    basis_now = jax.scipy.linalg.solve_triangular(factor, spread, lower=True)
    offset = lax.axis_index(CELLS) * share_cols
    result = lax.dynamic_slice_in_dim(basis_now, offset, share_cols, 1)
    return result * math.sqrt(gene_count * lax.axis_size("genes"))


def solution(mesh):
    split = Mesh(
        mesh.devices.reshape(16, 2, 4, mesh.shape["genes"]),
        ("cells_0", "cells_1", "cells_2", "genes"),
    )
    placed = (P(CELLS, "genes"), P(CELLS, "genes"), P(None, "genes"))
    return jax.shard_map(
        on_device, mesh=split, in_specs=placed, out_specs=P(None, GENES_CELLS), check_vma=False
    )
```

profile of v0, /device:TPU:1, one launch (start us, length us, event | category | flops | bytes accessed | tf_op | source)
XLA Modules:
  0.0 186.1 jit_solution(16931770004148447396)
XLA Ops:
  0.0 0.8 convert_bitcast_fusion
  0.9 2.1 %fusion = f32[4096]{0:T(1024)S(1)} fusion(bf16[128,4096]{1,0:T(8,128)(2,1)} %param.3, f32[4096]{0:T(1024)S(1)} %broadcast_bitcast_fusion), kind=kLoop, calls=%fused_computation.2 | loop fusion | flops 1568768 | bytes 1081344 | tf_op jit(solution)/shard_map/reduce_sum | solution.py:82
  3.0 9.3 %all_to_all.50 = f32[4,1,4096]{2,1,0:T(1,128)S(1)} all-to-all(f32[4,1,4096]{2,1,0:T(1,128)S(1)} %broadcast_in_dim.22), channel_id=1, replica_groups=mesh['cells_0'=16,'cells_1'=2,'cells_2'=4,'genes'=4] {'cells_2'}, dimensions={0} | all-to-all | bytes 131072 | tf_op jit(solution)/shard_map/all_to_all | solution.py:15
  12.3 0.5 broadcast_in_dim.23
  12.8 47.8 %all_to_all.51 = f32[32,1,4096]{2,1,0:T(1,128)S(1)} all-to-all(f32[32,1,4096]{2,1,0:T(1,128)S(1)} %broadcast_in_dim.23), channel_id=1, replica_groups=mesh['cells_0'=16,'cells_1'=2,'cells_2'=4,'genes'=4] {'cells_0','cells_1'}, dimensions={0} | all-to-all | bytes 1048576 | tf_op jit(solution)/shard_map/all_to_all | solution.py:15
  60.5 0.4 reduce_sum.65
  60.9 1.0 convolution_bitcast_fusion
  62.0 9.6 %all_to_all.52 = f32[4,64,128]{2,1,0:T(8,128)S(1)} all-to-all(f32[4,64,128]{2,1,0:T(8,128)S(1)} %broadcast_in_dim.24), channel_id=1, replica_groups=mesh['cells_0'=16,'cells_1'=2,'cells_2'=4,'genes'=4] {'genes'}, dimensions={0} | all-to-all | bytes 262144 | tf_op jit(solution)/shard_map/all_to_all | solution.py:15
  71.6 1.1 fusion.1
  72.9 0.5 reshape_reshape_reshape.6
  73.4 0.6 copy.22
  74.0 16.6 %all_to_all.53 = f32[4,32,2048]{2,1,0:T(8,128)S(1)} all-to-all(f32[4,32,2048]{2,1,0:T(8,128)S(1)} %bitcast.26), channel_id=1, replica_groups=mesh['cells_0'=16,'cells_1'=2,'cells_2'=4,'genes'=4] {'cells_2'}, dimensions={0} | all-to-all | bytes 2097152 | tf_op jit(solution)/shard_map/all_to_all | solution.py:34
  90.6 0.2 all_to_all.36
  90.8 23.7 %all_to_all.54 = f32[32,1,2048]{2,1,0:T(1,128)S(1)} all-to-all(f32[32,1,2048]{2,1,0:T(1,128)S(1)} %all_to_all.36), channel_id=1, replica_groups=mesh['cells_0'=16,'cells_1'=2,'cells_2'=4,'genes'=4] {'cells_0','cells_1'}, dimensions={0} | all-to-all | bytes 524288 | tf_op jit(solution)/shard_map/all_to_all | solution.py:41
  114.6 0.2 reduce_sum.68
  114.7 0.1 broadcast_in_dim.25
  114.9 25.3 %all_to_all.55 = f32[32,1,2048]{2,1,0:T(1,128)S(1)} all-to-all(f32[32,1,2048]{2,1,0:T(1,128)S(1)} %broadcast_in_dim.25), channel_id=1, replica_groups=mesh['cells_0'=16,'cells_1'=2,'cells_2'=4,'genes'=4] {'cells_0','cells_1'}, dimensions={0} | all-to-all | bytes 524288 | tf_op jit(solution)/shard_map/all_to_all | solution.py:15
  140.4 13.8 %all_to_all.56 = f32[4,32,2048]{2,1,0:T(8,128)S(1)} all-to-all(f32[4,32,2048]{2,1,0:T(8,128)S(1)} %broadcast_in_dim.26), channel_id=1, replica_groups=mesh['cells_0'=16,'cells_1'=2,'cells_2'=4,'genes'=4] {'cells_2'}, dimensions={0} | all-to-all | bytes 2097152 | tf_op jit(solution)/shard_map/all_to_all | solution.py:15
  154.2 0.7 copy.15
  154.9 0.6 reshape_reshape_reshape.7
  155.5 1.0 fusion.10
  156.5 0.7 reshape.36
  157.3 7.9 %all-to-all-start.7 = ((f32[4,1,4096]{2,1,0:T(1,128)}), f32[4,1,4096]{2,1,0:T(1,128)S(1)}, u32[]{:S(2)}, u32[]{:S(2)}) async-start(f32[4,1,4096]{2,1,0:T(1,128)} %reshape.36), calls=%async_computation.7 | async-start | bytes 131072 | tf_op jit(solution)/shard_map/all_to_all | solution.py:15
  165.1 3.3 %all-to-all-done.7 = f32[4,1,4096]{2,1,0:T(1,128)S(1)} async-done(((f32[4,1,4096]{2,1,0:T(1,128)}), f32[4,1,4096]{2,1,0:T(1,128)S(1)}, u32[]{:S(2)}, u32[]{:S(2)}) %all-to-all-start.7) | async-done | bytes 65568 | tf_op jit(solution)/shard_map/all_to_all | solution.py:15
  168.4 0.5 broadcast.72
  168.9 0.8 reduce.9
  170.0 5.8 %cholesky.16 = f32[64,64]{1,0:T(8,128)S(1)} custom-call(f32[64,64]{1,0:T(8,128)S(1)} %fusion.8), custom_call_target="Cholesky" | custom-call | tf_op jit(solution)/shard_map/jit(cholesky)/cholesky | solution.py:104
  175.9 0.6 compare_reduce_fusion
  176.5 0.7 fusion.2
  177.2 4.9 %custom-call.7 = f32[1,64,64]{1,2,0:T(8,128)S(1)} custom-call(f32[1,64,64]{2,1,0:T(8,128)S(1)} %fusion.2), custom_call_target="InvertDiagBlocksLowerTriangular" | custom-call | tf_op jit(solution)/shard_map/jit(_solve_triangular)/triangular_solve | solution.py:105
  182.1 3.5 %fusion.6 = f32[64,4096]{0,1:T(8,128)S(1)} fusion(f32[64,4096]{1,0:T(8,128)S(1)} %reshape_reshape_reshape.7, f32[1,64,64]{1,2,0:T(8,128)S(1)} %custom-call.7), kind=kOutput, calls=%fused_computation.13 | convolution fusion | flops 201326592 | bytes 2113536 | tf_op jit(solution)/shard_map/jit(_solve_triangular)/triangular_solve | solution.py:105
  185.5 0.6 dynamic-slice_multiply_fusion
  (21 shorter events, 0.8 us)
Async XLA Ops:
  0.0 60.9 %copy-start = (bf16[64,4096]{1,0:T(8,128)(2,1)S(1)}, bf16[64,4096]{1,0:T(8,128)(2,1)}, u32[]{:S(2)}) copy-start(bf16[64,4096]{1,0:T(8,128)(2,1)} %param.5) | copy-start | bytes 1572868
  0.0 60.9 %copy-start.1 = (bf16[128,4096]{1,0:T(8,128)(2,1)S(1)}, bf16[128,4096]{1,0:T(8,128)(2,1)}, u32[]{:S(2)}) copy-start(bf16[128,4096]{1,0:T(8,128)(2,1)} %param.3) | copy-start | bytes 3145732
  157.3 11.1 %all-to-all-start.7 = ((f32[4,1,4096]{2,1,0:T(1,128)}), f32[4,1,4096]{2,1,0:T(1,128)S(1)}, u32[]{:S(2)}, u32[]{:S(2)}) async-start(f32[4,1,4096]{2,1,0:T(1,128)} %reshape.36), calls=%async_computation.7 | async-start | bytes 131072 | tf_op jit(solution)/shard_map/all_to_all | solution.py:15
where the time goes:
time: 187 us; the launch traced here: 186 us
  blocking collectives  146 us (78%)
  other arithmetic  17.1 us (9%)
  starting transfers between devices  7.87 us (4%)
  matrix products  6.56 us (4%)
  local copies, waits for them, and re-layouts  4.97 us (3%)
  waiting for transfers between devices  3.26 us (2%)
    all_to_all x5, blocking collectives, copy_for_each(): return lax.all_to_all(copies, axis, split_axis=0, concat_axis=0, tiled=True)  106 us
    all_to_all x1, blocking collectives, sum_by_axis(): return jnp.sum(lax.all_to_all(own, far, 0, 0, tiled=True), axis=0)  23.7 us
    all_to_all x1, blocking collectives, sent_and_summed(): lax.all_to_all(in_blocks(shard, dim, peers), axis, 0, 0, tiled=True)  16.6 us
    all_to_all x1, starting transfers between devices, copy_for_each(): return lax.all_to_all(copies, axis, split_axis=0, concat_axis=0, tiled=True)  7.87 us
    another operation x3, other arithmetic, on_device(): factor = jnp.linalg.cholesky(gram_sum)  6.52 us
    another operation x2, other arithmetic, on_device(): basis_now = jax.scipy.linalg.solve_triangular(factor, spread, lower=True)  5.55 us
  transfers between devices with their start and end apart: 1, of which 1 were waited for; matrix products, arithmetic and copies ran while one was open for 0% of the time, Pallas kernels for 0%

commit v1 on v0

v1 whole, which is shorter than its diff:
```python
import functools
import math

import jax
import jax.numpy as jnp
from jax import lax
from jax.experimental import pallas as pl
from jax.experimental.pallas import tpu as pltpu
from jax.sharding import PartitionSpec as P

F32 = jnp.float32
BF16 = jnp.bfloat16
MESH = pl.DeviceIdType.MESH
Z, H, Y, XL, CORE = 16, 2, 4, 2, 2
LANES = 128
OFFSETS = (8, 7, 9, 6, 10, 5, 11, 4, 12, 3, 13, 2, 14, 1, 15, 0)
CHUNKS = 4
NT = (((1,), (1,)), ((), ()))


def device(z, h, y, xl, core):
    return ((z * H + h) * Y + y, xl * CORE + core)


def total_of(values):
    values = list(values)
    while len(values) > 1:
        values = [sum(values[i : i + 2][1:], values[i]) for i in range(0, len(values), 2)]
    return values[0]


def solve(gram, right):
    blocks = gram.shape[0] // 8
    left = [gram[8 * b : 8 * b + 8] for b in range(blocks)]
    right = [right[8 * b : 8 * b + 8] for b in range(blocks)]
    row_at = lax.broadcasted_iota(jnp.int32, (8, LANES), 0)
    done = []
    for kb in range(blocks):
        cols = [
            [
                jnp.broadcast_to(left[b][:, 8 * kb + j : 8 * kb + j + 1], (8, LANES))
                for j in range(8)
            ]
            for b in range(kb, blocks)
        ]
        rows_left, rows_right = left[kb], right[kb]
        scale = jnp.zeros((8, LANES), F32)
        steps = []
        for j in range(8):
            pivot = jnp.broadcast_to(cols[0][j][j : j + 1], (8, LANES))
            inv = lax.rsqrt(pivot)
            scale = jnp.where(row_at == j, inv, scale)
            lower = [c[j] * inv for c in cols]
            for m in range(j + 1, 8):
                entry = jnp.broadcast_to(lower[0][m : m + 1], (8, LANES))
                for c, low in zip(cols, lower):
                    c[m] = c[m] - low * entry
            below = jnp.where(row_at > j, lower[0], 0.0)
            unit_left = jnp.broadcast_to(rows_left[j : j + 1], rows_left.shape) * inv[:, : rows_left.shape[1]]
            unit_right = jnp.broadcast_to(rows_right[j : j + 1], rows_right.shape) * inv
            rows_left = rows_left - below[:, : rows_left.shape[1]] * unit_left
            rows_right = rows_right - below * unit_right
            steps.append((lower[1:], unit_left, unit_right))
        done.append(rows_right * scale)
        for at, b in enumerate(range(kb + 1, blocks)):
            for lower, unit_left, unit_right in steps:
                left[b] = left[b] - lower[at][:, : unit_left.shape[1]] * unit_left
                right[b] = right[b] - lower[at] * unit_right
    return jnp.concatenate(done, axis=0)


def kernel(
    scaling,
    counts,
    occupancy,
    basis,
    out,
    cbuf,
    split_mean,
    aux,
    aux_in,
    score,
    score_in,
    part,
    part_in,
    dev_mean,
    mean_xy,
    turned,
    zpart,
    zaux,
    zpart_in,
    zaux_in,
    tile,
    gram,
    gram_in,
    gram_z,
    gram_z_in,
    gram_all,
    sem_score,
    sem_aux,
    sem_part,
    sem_z,
    sem_zaux,
    sem_tile,
    sem_gram,
    sem_gram_z,
    sem_core,
):
    cells_at, genes_at = lax.axis_index("cells"), lax.axis_index("genes")
    z, h, y = cells_at // (H * Y), lax.rem(cells_at // Y, H), lax.rem(cells_at, Y)
    xl, core = genes_at // CORE, lax.rem(genes_at, CORE)
    comps = basis.shape[0]
    rows = comps // Y
    cells = counts.shape[0]

    def send(src, dst, sems, index, to):
        copy = pltpu.make_async_remote_copy(
            src_ref=src,
            dst_ref=dst,
            send_sem=sems.at[(0, *index)],
            recv_sem=sems.at[(1, *index)],
            device_id=to,
            device_id_type=MESH,
        )
        copy.start()
        return copy

    def gene_peer(a):
        other = lax.rem(genes_at + a, XL * CORE)
        return device(z, h, y, other // CORE, lax.rem(other, CORE))

    def xy_place(a, b):
        return lax.rem(h + a, H), lax.rem(y + b, Y)

    def z_peer(o):
        return device(lax.rem(z + o, Z), h, y, xl, core)

    def x_peer(a):
        other = lax.rem((h * XL + xl) * CORE + core + a, H * XL * CORE)
        return device(
            z, other // (XL * CORE), y, lax.rem(other // CORE, XL), lax.rem(other, CORE)
        )

    xy_offsets = [(a, b) for a in range(H) for b in range(Y) if a or b]

    barrier = pltpu.get_barrier_semaphore()
    peers = [gene_peer(a) for a in range(1, XL * CORE)]
    peers += [device(z, *xy_place(a, b), xl, core) for a, b in xy_offsets]
    peers += [z_peer(o) for o in range(1, Z)]
    for a in range(1, XL * CORE):
        other = lax.rem(genes_at + a, XL * CORE)
        peers.append(device(z, 1 - h, y, other // CORE, lax.rem(other, CORE)))
    for peer in peers:
        pl.semaphore_signal(barrier, inc=1, device_id=peer, device_id_type=MESH)

    row_at = lax.broadcasted_iota(jnp.int32, (16, LANES), 0)
    aux[:, 16:24, :] = jnp.zeros((H, 8, LANES), F32)

    def center(zt, carry):
        for ht in range(H):
            at = pl.multiple_of((zt * H + ht) * LANES, LANES)
            entries = counts[:, pl.ds(at, LANES)].astype(F32)
            stored = occupancy[0, zt * H + ht].astype(F32)
            logged = jnp.log(1.0 + entries) * stored
            mean = jnp.sum(logged, axis=0, keepdims=True) * (1.0 / cells)
            cbuf[:, pl.ds(at, LANES)] = (logged - mean).astype(BF16)
            aux[ht, pl.ds(zt, 1), :] = mean
            high = mean.astype(BF16).astype(F32)
            middle = (mean - high).astype(BF16).astype(F32)
            low = mean - high - middle
            stacked = jnp.where(
                row_at == 0, high, jnp.where(row_at == 1, middle, jnp.where(row_at == 2, low, 0.0))
            )
            split_mean[:, pl.ds(at, LANES)] = stacked.astype(BF16)
        return carry

    lax.fori_loop(0, Z, center, 0)

    score[0:comps, :] = lax.dot_general(basis[...], cbuf[...], NT, preferred_element_type=F32)
    of_mean = lax.dot_general(split_mean[...], basis[...], NT, preferred_element_type=F32)
    score[comps : comps + 8, :] = jnp.zeros((8, LANES), F32)
    score[comps : comps + 1, 0:comps] = of_mean[0:1] + of_mean[1:2] + of_mean[2:3]

    pl.semaphore_wait(barrier, len(peers))
    copies = [
        send(score, score_in.at[a - 1], sem_score, (a - 1,), gene_peer(a))
        for a in range(1, XL * CORE)
    ]
    for copy in copies:
        copy.wait()
    whole = total_of([score[...]] + [score_in[a] for a in range(XL * CORE - 1)])
    scores, own_mean = whole[0:comps], whole[comps : comps + 1]
    for ht in range(H):
        aux[ht, 16:17, :] = own_mean

    aux_copies = []
    for s, (a, b) in enumerate(xy_offsets):
        ht, yt = xy_place(a, b)
        aux_copies.append(
            send(aux.at[ht], aux_in.at[s], sem_aux, (s,), device(z, ht, yt, xl, core))
        )

    score_high = scores.astype(BF16)
    score_low = (scores - score_high.astype(F32)).astype(BF16)
    stacked = jnp.concatenate([score_high, score_low], axis=0)
    per_chunk = Z // CHUNKS
    part_copies = []
    for chunk in range(CHUNKS):
        span = pl.ds(chunk * per_chunk, per_chunk)
        for i in range(chunk * per_chunk, (chunk + 1) * per_chunk):
            zt = lax.rem(z + OFFSETS[i], Z)
            at = pl.multiple_of(zt * (H * LANES), H * LANES)
            both = jnp.dot(stacked, cbuf[:, pl.ds(at, H * LANES)], preferred_element_type=F32)
            product = both[:comps] + both[comps:]
            for ht in range(H):
                for yt in range(Y):
                    part[ht, yt, i] = product[
                        yt * rows : (yt + 1) * rows, ht * LANES : (ht + 1) * LANES
                    ]
        sent = []
        for s, (a, b) in enumerate(xy_offsets):
            ht, yt = xy_place(a, b)
            sent.append(
                send(
                    part.at[ht, yt, span],
                    part_in.at[s, span],
                    sem_part,
                    (s, chunk),
                    device(z, ht, yt, xl, core),
                )
            )
        part_copies.append(sent)

    def deviations(weight, means):
        middle = total_of(means) * (1.0 / len(means))
        turned[...] = jnp.zeros((LANES, LANES), F32)
        for p, value in enumerate(means):
            turned[p : p + 1, :] = (value - middle) * weight
        turned[...] = turned[...].T
        own = turned[pl.ds(pl.multiple_of(y * rows, rows), rows), :]
        return middle, [
            jnp.broadcast_to(own[:, p : p + 1], (rows, LANES)) for p in range(len(means))
        ]

    for copy in aux_copies:
        copy.wait()
    groups = len(xy_offsets) + 1
    score_xy, away = deviations(
        float(cells), [own_mean] + [aux_in[s, 16:17, :] for s in range(groups - 1)]
    )
    means = [aux[h, 0:16, :]] + [aux_in[s, 0:16, :] for s in range(groups - 1)]
    middle = total_of(means) * (1.0 / groups)
    mean_xy[...] = middle
    for p, value in enumerate(means):
        dev_mean[p] = value - middle

    z_copies = []
    for chunk in range(CHUNKS):
        for copy in part_copies[chunk]:
            copy.wait()
        for i in range(chunk * per_chunk, (chunk + 1) * per_chunk):
            zt = lax.rem(z + OFFSETS[i], Z)
            terms = [part[h, y, i]] + [part_in[s, i] for s in range(groups - 1)]
            terms += [away[p] * dev_mean[p, pl.ds(zt, 1), :] for p in range(groups)]
            zpart[i] = total_of(terms)
            zaux[i, 0:1, :] = mean_xy[pl.ds(zt, 1), :]
            zaux[i, 1:2, :] = score_xy
            if OFFSETS[i]:
                to = z_peer(OFFSETS[i])
                z_copies.append(send(zpart.at[i], zpart_in.at[i], sem_z, (i,), to))
                z_copies.append(send(zaux.at[i], zaux_in.at[i], sem_zaux, (i,), to))
    for copy in z_copies:
        copy.wait()
    _, away = deviations(
        float(cells * groups), [zaux[Z - 1, 1:2, :]] + [zaux_in[i, 1:2, :] for i in range(Z - 1)]
    )
    means = [zaux[Z - 1, 0:1, :]] + [zaux_in[i, 0:1, :] for i in range(Z - 1)]
    middle = total_of(means) * (1.0 / Z)
    terms = [zpart[Z - 1]] + [zpart_in[i] for i in range(Z - 1)]
    terms += [far * (value - middle) for far, value in zip(away, means)]
    tile[y] = total_of(terms)

    copies = [
        send(tile.at[y], tile.at[y], sem_tile, (b - 1,), device(z, h, lax.rem(y + b, Y), xl, core))
        for b in range(1, Y)
    ]
    for copy in copies:
        copy.wait()
    spread = tile[...].reshape(comps, LANES)
    own_gram = lax.dot_general(
        spread, spread, NT, precision=lax.Precision.HIGHEST, preferred_element_type=F32
    )
    half = comps // 2
    gram[:, 0:comps] = own_gram[0:half]
    gram[:, comps : 2 * comps] = own_gram[half:]
    along_x = H * XL * CORE
    copies = [send(gram, gram_in.at[a - 1], sem_gram, (a - 1,), x_peer(a)) for a in range(1, along_x)]
    spread = pltpu.roll(spread, lax.rem((Y - y) * (LANES // Y), LANES), 1)
    for copy in copies:
        copy.wait()
    quarter = half // CORE
    here = pl.ds(pl.multiple_of(core * quarter, quarter), quarter)
    gram_z[...] = total_of([gram[here, :]] + [gram_in[a, here, :] for a in range(along_x - 1)])
    copies = [
        send(gram_z, gram_z_in.at[o - 1], sem_gram_z, (o - 1,), z_peer(o)) for o in OFFSETS[: Z - 1]
    ]
    for copy in copies:
        copy.wait()
    gram_all[core] = total_of([gram_z[...]] + [gram_z_in[o] for o in range(Z - 1)])
    send(gram_all.at[core], gram_all.at[core], sem_core, (0,), device(z, h, y, xl, 1 - core)).wait()
    packed = gram_all[...].reshape(half, LANES)
    gram_sum = jnp.concatenate([packed[:, 0:comps], packed[:, comps : 2 * comps]], axis=0)
    result = solve(gram_sum, spread)
    out[...] = result[:, 0 : LANES // Y] * scaling


def on_device(counts, occupancy, start_basis):
    comps, genes = start_basis.shape
    cells = counts.shape[0]
    rows = comps // Y
    scaling = math.sqrt(genes * XL * CORE)
    dma = pltpu.SemaphoreType.DMA
    vmem = pl.BlockSpec(memory_space=pltpu.VMEM)
    return pl.pallas_call(
        functools.partial(kernel, scaling),
        out_shape=jax.ShapeDtypeStruct((comps, LANES // Y), F32),
        in_specs=[vmem, pl.BlockSpec(memory_space=pltpu.SMEM), vmem],
        out_specs=vmem,
        scratch_shapes=[
            pltpu.VMEM((cells, genes), BF16),
            pltpu.VMEM((16, genes), BF16),
            pltpu.VMEM((H, 24, LANES), F32),
            pltpu.VMEM((H * Y - 1, 24, LANES), F32),
            pltpu.VMEM((comps + 8, LANES), F32),
            pltpu.VMEM((XL * CORE - 1, comps + 8, LANES), F32),
            pltpu.VMEM((H, Y, Z, rows, LANES), F32),
            pltpu.VMEM((H * Y - 1, Z, rows, LANES), F32),
            pltpu.VMEM((H * Y, Z, LANES), F32),
            pltpu.VMEM((Z, LANES), F32),
            pltpu.VMEM((LANES, LANES), F32),
            pltpu.VMEM((Z, rows, LANES), F32),
            pltpu.VMEM((Z, 2, LANES), F32),
            pltpu.VMEM((Z - 1, rows, LANES), F32),
            pltpu.VMEM((Z - 1, 2, LANES), F32),
            pltpu.VMEM((Y, rows, LANES), F32),
            pltpu.VMEM((comps // 2, LANES), F32),
            pltpu.VMEM((H * XL * CORE - 1, comps // 2, LANES), F32),
            pltpu.VMEM((comps // 2 // CORE, LANES), F32),
            pltpu.VMEM((Z - 1, comps // 2 // CORE, LANES), F32),
            pltpu.VMEM((CORE, comps // 2 // CORE, LANES), F32),
            dma((2, XL * CORE - 1)),
            dma((2, H * Y - 1)),
            dma((2, H * Y - 1, CHUNKS)),
            dma((2, Z - 1)),
            dma((2, Z - 1)),
            dma((2, Y - 1)),
            dma((2, H * XL * CORE - 1)),
            dma((2, Z - 1)),
            dma((2, 1)),
        ],
        compiler_params=pltpu.CompilerParams(collective_id=0, has_side_effects=True),
        name="subspace_step",
    )(counts, occupancy, start_basis)


def solution(mesh):
    placed = (P("cells", "genes"), P("cells", "genes"), P(None, "genes"))
    return jax.shard_map(
        on_device, mesh=mesh, in_specs=placed, out_specs=P(None, ("genes", "cells")), check_vma=False
    )
```

time: 187 us -> 64.4 us (0.34)
  blocking collectives: 146 us -> 0 us
  Pallas kernels: 0 us -> 62.7 us
  other arithmetic: 17.1 us -> 0 us
  starting transfers between devices: 7.87 us -> 0 us
  matrix products: 6.56 us -> 0 us
  local copies, waits for them, and re-layouts: 4.97 us -> 1.44 us
  waiting for transfers between devices: 3.26 us -> 0 us
    all_to_all x7 -> x0, blocking collectives: 146 us -> none  [the longest x5 106 us: copy_for_each(): return lax.all_to_all(copies, axis, split_axis=0, concat_axis=0, tiled=True)]
    pallas_call x0 -> x1, Pallas kernels: none -> 62.7 us  [on_device(): pl.pallas_call(functools.partial(kernel, scaling), out_shape=jax.ShapeDty...]
    another operation x5 -> x0, other arithmetic: 12.1 us -> none  [the longest x3 6.52 us: on_device(): factor = jnp.linalg.cholesky(gram_sum)]
    all_to_all x1 -> x0, starting transfers between devices: 7.87 us -> none  [copy_for_each(): return lax.all_to_all(copies, axis, split_axis=0, concat_axis=0, tiled=True)]
    another operation x1 -> x0, matrix products: 3.46 us -> none  [on_device(): basis_now = jax.scipy.linalg.solve_triangular(factor, spread, lower=True)]
    all_to_all x1 -> x0, waiting for transfers between devices: 3.26 us -> none  [copy_for_each(): return lax.all_to_all(copies, axis, split_axis=0, concat_axis=0, tiled=True)]
    dot_general x3 -> x0, matrix products: 3.1 us -> none  [the longest x1 1.14 us: on_device(): both = jnp.dot(stacked, centered, preferred_element_type=jnp.float32)]
    reduce_sum x7 -> x0, other arithmetic: 2.74 us -> none  [the longest x1 2.07 us: on_device(): jnp.sum(logged, axis=0)]
  transfers between devices with their start and end apart: 1 -> 0, of which waited for: 1 -> 0; matrix products, arithmetic and copies ran while one was open for 0% -> 0% of each run, Pallas kernels for 0% -> 0%
where the time goes in v1:
time: 64.4 us; the launch traced here: 64.2 us
  Pallas kernels  62.7 us (97%)
  local copies, waits for them, and re-layouts  1.44 us (2%)
    pallas_call x1, Pallas kernels, on_device(): pl.pallas_call(functools.partial(kernel, scaling), out_shape=jax.ShapeDty...  62.7 us
    pallas_call x1, local copies, waits for them, and re-layouts, on_device(): pl.pallas_call(functools.partial(kernel, scaling), out_shape=jax.ShapeDty...  1.44 us

profile of v1, /device:TPU:1, one launch (start us, length us, event | category | flops | bytes accessed | tf_op | source)
XLA Modules:
  0.0 64.2 jit_solution(13590173042325006478)
XLA Ops:
  0.0 62.7 %subspace_step.1 = f32[64,32]{1,0:T(8,128)} custom-call(bf16[128,4096]{1,0:T(8,128)(2,1)} %counts.1, s32[1,32]{1,0:T(1,128)} %occupancy.1, bf16[64,4096]{1,0:T(8,128)(2,1)} %basis.1), custom_call_target="tpu_custom_call" | custom-call | tf_op jit(solution)/shard_map/subspace_step/pallas_call | solution.py:324
  62.7 1.4 %copy.4 = f32[64,32]{0,1:T(8,128)} copy(f32[64,32]{1,0:T(8,128)} %subspace_step.1) | data formatting | bytes 16384 | tf_op jit(solution)/shard_map/subspace_step/pallas_call | solution.py:324

commit v2 on v1

--- a/solution.py
+++ b/solution.py
@@ -1,4 +1,3 @@
-import functools
 import math
 
 import jax
@@ -15,6 +14,7 @@
 LANES = 128
 OFFSETS = (8, 7, 9, 6, 10, 5, 11, 4, 12, 3, 13, 2, 14, 1, 15, 0)
 CHUNKS = 4
+NEAR = 4
 NT = (((1,), (1,)), ((), ()))
 
 
@@ -70,11 +70,13 @@
 
 
 def kernel(
-    scaling,
+    counts_hbm,
+    occupancy_hbm,
+    basis_hbm,
+    out,
     counts,
     occupancy,
     basis,
-    out,
     cbuf,
     split_mean,
     aux,
@@ -90,21 +92,21 @@
     zaux,
     zpart_in,
     zaux_in,
-    tile,
     gram,
     gram_in,
     gram_z,
     gram_z_in,
     gram_all,
+    sem_in,
     sem_score,
     sem_aux,
     sem_part,
     sem_z,
     sem_zaux,
-    sem_tile,
     sem_gram,
     sem_gram_z,
-    sem_core,
+    sem_all,
+    sem_far,
 ):
     cells_at, genes_at = lax.axis_index("cells"), lax.axis_index("genes")
     z, h, y = cells_at // (H * Y), lax.rem(cells_at // Y, H), lax.rem(cells_at, Y)
@@ -112,6 +114,17 @@
     comps = basis.shape[0]
     rows = comps // Y
     cells = counts.shape[0]
+    width = LANES // Y
+    plane = H * XL * CORE * Y
+
+    loads = [pltpu.make_async_copy(occupancy_hbm, occupancy, sem_in.at[0])]
+    wide = counts.shape[1] // CHUNKS
+    for c in range(CHUNKS):
+        span = pl.ds(c * wide, wide)
+        loads.append(pltpu.make_async_copy(counts_hbm.at[:, span], counts.at[:, span], sem_in.at[c + 1]))
+    loads.append(pltpu.make_async_copy(basis_hbm, basis, sem_in.at[CHUNKS + 1]))
+    for load in loads:
+        load.start()
 
     def send(src, dst, sems, index, to):
         copy = pltpu.make_async_remote_copy(
@@ -135,26 +148,32 @@
     def z_peer(o):
         return device(lax.rem(z + o, Z), h, y, xl, core)
 
-    def x_peer(a):
-        other = lax.rem((h * XL + xl) * CORE + core + a, H * XL * CORE)
+    place = ((h * XL + xl) * CORE + core) * Y + y
+
+    def plane_place(a):
+        return lax.rem(place + a, plane)
+
+    def plane_peer(a):
+        other = plane_place(a)
+        in_x = other // Y
         return device(
-            z, other // (XL * CORE), y, lax.rem(other // CORE, XL), lax.rem(other, CORE)
+            z, in_x // (XL * CORE), lax.rem(other, Y), lax.rem(in_x // CORE, XL), lax.rem(in_x, CORE)
         )
 
     xy_offsets = [(a, b) for a in range(H) for b in range(Y) if a or b]
 
     barrier = pltpu.get_barrier_semaphore()
+    near = [o for o in range(1, Z) if min(o, Z - o) <= NEAR]
     peers = [gene_peer(a) for a in range(1, XL * CORE)]
     peers += [device(z, *xy_place(a, b), xl, core) for a, b in xy_offsets]
-    peers += [z_peer(o) for o in range(1, Z)]
-    for a in range(1, XL * CORE):
-        other = lax.rem(genes_at + a, XL * CORE)
-        peers.append(device(z, 1 - h, y, other // CORE, lax.rem(other, CORE)))
+    peers += [z_peer(o) for o in near]
     for peer in peers:
         pl.semaphore_signal(barrier, inc=1, device_id=peer, device_id_type=MESH)
 
     row_at = lax.broadcasted_iota(jnp.int32, (16, LANES), 0)
+    group_at = lax.broadcasted_iota(jnp.int32, (16, LANES), 1) // width
     aux[:, 16:24, :] = jnp.zeros((H, 8, LANES), F32)
+    turned[...] = jnp.zeros((LANES, LANES), F32)
 
     def center(zt, carry):
         for ht in range(H):
@@ -174,7 +193,12 @@
             split_mean[:, pl.ds(at, LANES)] = stacked.astype(BF16)
         return carry
 
-    lax.fori_loop(0, Z, center, 0)
+    per_chunk = Z // CHUNKS
+    loads[0].wait()
+    for c in range(CHUNKS):
+        loads[c + 1].wait()
+        lax.fori_loop(c * per_chunk, (c + 1) * per_chunk, center, 0)
+    loads[-1].wait()
 
     score[0:comps, :] = lax.dot_general(basis[...], cbuf[...], NT, preferred_element_type=F32)
     of_mean = lax.dot_general(split_mean[...], basis[...], NT, preferred_element_type=F32)
@@ -182,6 +206,8 @@
     score[comps : comps + 1, 0:comps] = of_mean[0:1] + of_mean[1:2] + of_mean[2:3]
 
     pl.semaphore_wait(barrier, len(peers))
+    for o in (NEAR, Z - NEAR):
+        pl.semaphore_signal(sem_far, inc=1, device_id=z_peer(o), device_id_type=MESH)
     copies = [
         send(score, score_in.at[a - 1], sem_score, (a - 1,), gene_peer(a))
         for a in range(1, XL * CORE)
@@ -203,7 +229,6 @@
     score_high = scores.astype(BF16)
     score_low = (scores - score_high.astype(F32)).astype(BF16)
     stacked = jnp.concatenate([score_high, score_low], axis=0)
-    per_chunk = Z // CHUNKS
     part_copies = []
     for chunk in range(CHUNKS):
         span = pl.ds(chunk * per_chunk, per_chunk)
@@ -213,10 +238,15 @@
             both = jnp.dot(stacked, cbuf[:, pl.ds(at, H * LANES)], preferred_element_type=F32)
             product = both[:comps] + both[comps:]
             for ht in range(H):
+                turns = []
+                for b in range(Y):
+                    block = product[b * rows : (b + 1) * rows, ht * LANES : (ht + 1) * LANES]
+                    turns.append([block] + [pltpu.roll(block, k * width, 1) for k in range(1, Y)])
                 for yt in range(Y):
-                    part[ht, yt, i] = product[
-                        yt * rows : (yt + 1) * rows, ht * LANES : (ht + 1) * LANES
-                    ]
+                    piece = turns[0][(0 - yt) % Y]
+                    for b in range(1, Y):
+                        piece = jnp.where(group_at == b, turns[b][(b - yt) % Y], piece)
+                    part[ht, yt, i] = piece
         sent = []
         for s, (a, b) in enumerate(xy_offsets):
             ht, yt = xy_place(a, b)
@@ -233,14 +263,21 @@
 
     def deviations(weight, means):
         middle = total_of(means) * (1.0 / len(means))
-        turned[...] = jnp.zeros((LANES, LANES), F32)
         for p, value in enumerate(means):
             turned[p : p + 1, :] = (value - middle) * weight
-        turned[...] = turned[...].T
-        own = turned[pl.ds(pl.multiple_of(y * rows, rows), rows), :]
-        return middle, [
-            jnp.broadcast_to(own[:, p : p + 1], (rows, LANES)) for p in range(len(means))
-        ]
+        flat = turned[...].T
+        away = []
+        for p in range(len(means)):
+            folded = jnp.broadcast_to(flat[0:rows, p : p + 1], (rows, LANES))
+            for b in range(1, Y):
+                block = jnp.broadcast_to(flat[b * rows : (b + 1) * rows, p : p + 1], (rows, LANES))
+                folded = jnp.where(group_at == b, block, folded)
+            away.append(folded)
+        return middle, away
+
+    def own_columns(means):
+        kept = jnp.where(group_at == y, means, 0.0)
+        return total_of([kept] + [pltpu.roll(kept, k * width, 1) for k in range(1, Y)])
 
     for copy in aux_copies:
         copy.wait()
@@ -250,10 +287,11 @@
     )
     means = [aux[h, 0:16, :]] + [aux_in[s, 0:16, :] for s in range(groups - 1)]
     middle = total_of(means) * (1.0 / groups)
-    mean_xy[...] = middle
+    mean_xy[...] = own_columns(middle)
     for p, value in enumerate(means):
-        dev_mean[p] = value - middle
-
+        dev_mean[p] = own_columns(value - middle)
+
+    pl.semaphore_wait(sem_far, 2)
     z_copies = []
     for chunk in range(CHUNKS):
         for copy in part_copies[chunk]:
@@ -278,55 +316,59 @@
     middle = total_of(means) * (1.0 / Z)
     terms = [zpart[Z - 1]] + [zpart_in[i] for i in range(Z - 1)]
     terms += [far * (value - middle) for far, value in zip(away, means)]
-    tile[y] = total_of(terms)
-
-    copies = [
-        send(tile.at[y], tile.at[y], sem_tile, (b - 1,), device(z, h, lax.rem(y + b, Y), xl, core))
-        for b in range(1, Y)
-    ]
-    for copy in copies:
-        copy.wait()
-    spread = tile[...].reshape(comps, LANES)
+    folded = total_of(terms)
+
+    blocks = [folded] + [pltpu.roll(folded, (Y - b) * width, 1) for b in range(1, Y)]
+    spread = jnp.concatenate([jnp.where(group_at == 0, block, 0.0) for block in blocks], axis=0)
     own_gram = lax.dot_general(
         spread, spread, NT, precision=lax.Precision.HIGHEST, preferred_element_type=F32
     )
-    half = comps // 2
-    gram[:, 0:comps] = own_gram[0:half]
-    gram[:, comps : 2 * comps] = own_gram[half:]
-    along_x = H * XL * CORE
-    copies = [send(gram, gram_in.at[a - 1], sem_gram, (a - 1,), x_peer(a)) for a in range(1, along_x)]
-    spread = pltpu.roll(spread, lax.rem((Y - y) * (LANES // Y), LANES), 1)
-    for copy in copies:
-        copy.wait()
-    quarter = half // CORE
-    here = pl.ds(pl.multiple_of(core * quarter, quarter), quarter)
-    gram_z[...] = total_of([gram[here, :]] + [gram_in[a, here, :] for a in range(along_x - 1)])
-    copies = [
-        send(gram_z, gram_z_in.at[o - 1], sem_gram_z, (o - 1,), z_peer(o)) for o in OFFSETS[: Z - 1]
-    ]
-    for copy in copies:
-        copy.wait()
-    gram_all[core] = total_of([gram_z[...]] + [gram_z_in[o] for o in range(Z - 1)])
-    send(gram_all.at[core], gram_all.at[core], sem_core, (0,), device(z, h, y, xl, 1 - core)).wait()
-    packed = gram_all[...].reshape(half, LANES)
+    packed = jnp.concatenate([own_gram[0:plane], own_gram[plane:]], axis=1)
+    for e in range(plane):
+        gram[e] = packed[e : e + 1]
+    for a in range(1, plane):
+        send(gram.at[plane_place(a)], gram_in.at[a - 1], sem_gram, (), plane_peer(a))
+    all_of(gram.at[pl.ds(0, plane - 1)], gram_in, sem_gram)
+    gram_z[...] = jnp.sum(gram_in[...], axis=0) + gram[place]
+    for a, o in enumerate(OFFSETS[: Z - 1]):
+        send(gram_z, gram_z_in.at[a], sem_gram_z, (), z_peer(o))
+    all_of(gram_z_in, gram_z_in, sem_gram_z)
+    gram_all[place] = jnp.sum(gram_z_in[...], axis=0) + gram_z[...]
+    for a in range(1, plane):
+        send(gram_all.at[place], gram_all.at[place], sem_all, (), plane_peer(a))
+    all_of(gram_all.at[pl.ds(0, plane - 1)], gram_all.at[pl.ds(0, plane - 1)], sem_all)
+    packed = gram_all[...].reshape(plane, LANES)
     gram_sum = jnp.concatenate([packed[:, 0:comps], packed[:, comps : 2 * comps]], axis=0)
-    result = solve(gram_sum, spread)
-    out[...] = result[:, 0 : LANES // Y] * scaling
+    out[...] = solve(gram_sum, spread).T[0:width]
+
+
+def all_of(sent, received, sems):
+    pltpu.make_async_remote_copy(
+        src_ref=sent,
+        dst_ref=received,
+        send_sem=sems.at[0],
+        recv_sem=sems.at[1],
+        device_id=(0, 0),
+        device_id_type=MESH,
+    ).wait()
 
 
 def on_device(counts, occupancy, start_basis):
     comps, genes = start_basis.shape
     cells = counts.shape[0]
     rows = comps // Y
-    scaling = math.sqrt(genes * XL * CORE)
+    plane = H * XL * CORE * Y
     dma = pltpu.SemaphoreType.DMA
-    vmem = pl.BlockSpec(memory_space=pltpu.VMEM)
-    return pl.pallas_call(
-        functools.partial(kernel, scaling),
-        out_shape=jax.ShapeDtypeStruct((comps, LANES // Y), F32),
-        in_specs=[vmem, pl.BlockSpec(memory_space=pltpu.SMEM), vmem],
-        out_specs=vmem,
+    hbm = pl.BlockSpec(memory_space=pltpu.HBM)
+    basis_now = pl.pallas_call(
+        kernel,
+        out_shape=jax.ShapeDtypeStruct((LANES // Y, comps), F32),
+        in_specs=[hbm, hbm, hbm],
+        out_specs=pl.BlockSpec(memory_space=pltpu.VMEM),
         scratch_shapes=[
+            pltpu.VMEM((cells, genes), BF16),
+            pltpu.SMEM(occupancy.shape, jnp.int32),
+            pltpu.VMEM((comps, genes), BF16),
             pltpu.VMEM((cells, genes), BF16),
             pltpu.VMEM((16, genes), BF16),
             pltpu.VMEM((H, 24, LANES), F32),
@@ -342,25 +384,28 @@
             pltpu.VMEM((Z, 2, LANES), F32),
             pltpu.VMEM((Z - 1, rows, LANES), F32),
             pltpu.VMEM((Z - 1, 2, LANES), F32),
-            pltpu.VMEM((Y, rows, LANES), F32),
-            pltpu.VMEM((comps // 2, LANES), F32),
-            pltpu.VMEM((H * XL * CORE - 1, comps // 2, LANES), F32),
-            pltpu.VMEM((comps // 2 // CORE, LANES), F32),
-            pltpu.VMEM((Z - 1, comps // 2 // CORE, LANES), F32),
-            pltpu.VMEM((CORE, comps // 2 // CORE, LANES), F32),
+            pltpu.VMEM((plane, 1, LANES), F32),
+            pltpu.VMEM((plane - 1, 1, LANES), F32),
+            pltpu.VMEM((1, LANES), F32),
+            pltpu.VMEM((Z - 1, 1, LANES), F32),
+            pltpu.VMEM((plane, 1, LANES), F32),
+            dma((CHUNKS + 2,)),
             dma((2, XL * CORE - 1)),
             dma((2, H * Y - 1)),
             dma((2, H * Y - 1, CHUNKS)),
             dma((2, Z - 1)),
             dma((2, Z - 1)),
-            dma((2, Y - 1)),
-            dma((2, H * XL * CORE - 1)),
-            dma((2, Z - 1)),
-            dma((2, 1)),
+            dma((2,)),
+            dma((2,)),
+            dma((2,)),
+            pltpu.SemaphoreType.REGULAR,
         ],
-        compiler_params=pltpu.CompilerParams(collective_id=0, has_side_effects=True),
+        compiler_params=pltpu.CompilerParams(
+            collective_id=0, has_side_effects=True, vmem_limit_bytes=24 << 20
+        ),
         name="subspace_step",
-    )(counts, occupancy, start_basis)
+    )(*(pltpu.with_memory_space_constraint(a, pltpu.HBM) for a in (counts, occupancy, start_basis)))
+    return basis_now.T * math.sqrt(genes * XL * CORE)
 
 
 def solution(mesh):

time: 64.4 us -> 59.2 us (0.919)
  Pallas kernels: 62.7 us -> 58.5 us
  local copies, waits for them, and re-layouts: 1.44 us -> 0 us
    pallas_call x1, Pallas kernels: 62.7 us -> 58.5 us  [on_device(): pl.pallas_call(kernel, out_shape=jax.ShapeDtypeStruct((LANES // Y, comps)...]
    pallas_call x1 -> x0, local copies, waits for them, and re-layouts: 1.44 us -> none  [on_device(): pl.pallas_call(functools.partial(kernel, scaling), out_shape=jax.ShapeDty...]
where the time goes in v2:
time: 59.2 us; the launch traced here: 59.1 us
  Pallas kernels  58.5 us (99%)
  other arithmetic  0.61 us (1%)
    pallas_call x1, Pallas kernels, on_device(): pl.pallas_call(kernel, out_shape=jax.ShapeDtypeStruct((LANES // Y, comps)...  58.5 us

profile of v2, /device:TPU:1, one launch (start us, length us, event | category | flops | bytes accessed | tf_op | source)
XLA Modules:
  0.0 59.1 jit_solution(12376814991007924217)
XLA Ops:
  0.0 58.5 %subspace_step.1 = f32[32,64]{1,0:T(8,128)S(1)} custom-call(bf16[128,4096]{1,0:T(8,128)(2,1)} %counts_hbm.1, s32[1,32]{1,0:T(1,128)} %occupancy_hbm.1, bf16[64,4096]{1,0:T(8,128)(2,1)} %basis_hbm.1), custom_call_target="tpu_custom_call" | custom-call | tf_op jit(solution)/shard_map/subspace_step/pallas_call | solution.py:363
  58.5 0.6 %multiply_bitcast_fusion = f32[64,32]{0,1:T(8,128)} fusion(f32[32,64]{1,0:T(8,128)S(1)} %subspace_step.1), kind=kLoop, calls=%fused_computation | loop fusion | flops 2048 | bytes 16384 | tf_op jit(solution)/shard_map/mul | solution.py:408

commit v3 on v2

--- a/solution.py
+++ b/solution.py
@@ -12,7 +12,9 @@
 MESH = pl.DeviceIdType.MESH
 Z, H, Y, XL, CORE = 16, 2, 4, 2, 2
 LANES = 128
-OFFSETS = (8, 7, 9, 6, 10, 5, 11, 4, 12, 3, 13, 2, 14, 1, 15, 0)
+DIRECT = (8, 6, 10)
+PAIRED = (4, 12, 2, 14, 0)
+PAIRED_CHUNKS = ((0, 2), (2, 5))
 CHUNKS = 4
 NEAR = 4
 NT = (((1,), (1,)), ((), ()))
@@ -83,8 +85,16 @@
     aux_in,
     score,
     score_in,
-    part,
-    part_in,
+    aux_pair,
+    aux_pair_in,
+    aux_paired_in,
+    direct,
+    direct_in,
+    paired,
+    paired_in,
+    pair_out,
+    pair_in,
+    pair_dev,
     dev_mean,
     mean_xy,
     turned,
@@ -100,7 +110,11 @@
     sem_in,
     sem_score,
     sem_aux,
-    sem_part,
+    sem_aux_pair,
+    sem_aux_paired,
+    sem_direct,
+    sem_pair,
+    sem_paired,
     sem_z,
     sem_zaux,
     sem_gram,
@@ -146,7 +160,7 @@
         return lax.rem(h + a, H), lax.rem(y + b, Y)
 
     def z_peer(o):
-        return device(lax.rem(z + o, Z), h, y, xl, core)
+        return device(lax.rem(z + o + Z, Z), h, y, xl, core)
 
     place = ((h * XL + xl) * CORE + core) * Y + y
 
@@ -159,6 +173,12 @@
         return device(
             z, in_x // (XL * CORE), lax.rem(other, Y), lax.rem(in_x // CORE, XL), lax.rem(in_x, CORE)
         )
+
+    def z_tile(o):
+        return lax.rem(z + o + Z, Z)
+
+    beside = [1 - 2 * lax.rem(z + ht, 2) for ht in range(H)]
+    own_beside = 1 - 2 * lax.rem(z + h, 2)
 
     xy_offsets = [(a, b) for a in range(H) for b in range(Y) if a or b]
 
@@ -173,6 +193,7 @@
     row_at = lax.broadcasted_iota(jnp.int32, (16, LANES), 0)
     group_at = lax.broadcasted_iota(jnp.int32, (16, LANES), 1) // width
     aux[:, 16:24, :] = jnp.zeros((H, 8, LANES), F32)
+    aux_pair[:, 16:24, :] = jnp.zeros((H, 8, LANES), F32)
     turned[...] = jnp.zeros((LANES, LANES), F32)
 
     def center(zt, carry):
@@ -226,95 +247,187 @@
             send(aux.at[ht], aux_in.at[s], sem_aux, (s,), device(z, ht, yt, xl, core))
         )
 
+    pair_aux_copies = [
+        send(aux.at[ht], aux_pair_in.at[ht], sem_aux_pair, (ht,), z_peer(beside[ht])) for ht in range(H)
+    ]
+
     score_high = scores.astype(BF16)
     score_low = (scores - score_high.astype(F32)).astype(BF16)
     stacked = jnp.concatenate([score_high, score_low], axis=0)
-    part_copies = []
-    for chunk in range(CHUNKS):
-        span = pl.ds(chunk * per_chunk, per_chunk)
-        for i in range(chunk * per_chunk, (chunk + 1) * per_chunk):
-            zt = lax.rem(z + OFFSETS[i], Z)
-            at = pl.multiple_of(zt * (H * LANES), H * LANES)
-            both = jnp.dot(stacked, cbuf[:, pl.ds(at, H * LANES)], preferred_element_type=F32)
-            product = both[:comps] + both[comps:]
-            for ht in range(H):
-                turns = []
-                for b in range(Y):
-                    block = product[b * rows : (b + 1) * rows, ht * LANES : (ht + 1) * LANES]
-                    turns.append([block] + [pltpu.roll(block, k * width, 1) for k in range(1, Y)])
-                for yt in range(Y):
-                    piece = turns[0][(0 - yt) % Y]
-                    for b in range(1, Y):
-                        piece = jnp.where(group_at == b, turns[b][(b - yt) % Y], piece)
-                    part[ht, yt, i] = piece
+
+    def pieces(tiles):
+        columns = [
+            cbuf[:, pl.ds(pl.multiple_of((tiles[ht] * H + ht) * LANES, LANES), LANES)] for ht in range(H)
+        ]
+        both = jnp.dot(stacked, jnp.concatenate(columns, axis=1), preferred_element_type=F32)
+        product = both[:comps] + both[comps:]
+        result = []
+        for ht in range(H):
+            turns = []
+            for b in range(Y):
+                block = product[b * rows : (b + 1) * rows, ht * LANES : (ht + 1) * LANES]
+                turns.append([block] + [pltpu.roll(block, k * width, 1) for k in range(1, Y)])
+            for yt in range(Y):
+                piece = turns[0][(0 - yt) % Y]
+                for b in range(1, Y):
+                    piece = jnp.where(group_at == b, turns[b][(b - yt) % Y], piece)
+                result.append((ht, yt, piece))
+        return result
+
+    def exchange(src, dst, sems, chunk, span):
         sent = []
         for s, (a, b) in enumerate(xy_offsets):
             ht, yt = xy_place(a, b)
             sent.append(
                 send(
-                    part.at[ht, yt, span],
-                    part_in.at[s, span],
-                    sem_part,
+                    src.at[ht, yt, span],
+                    dst.at[s, span],
+                    sems,
                     (s, chunk),
                     device(z, ht, yt, xl, core),
                 )
             )
-        part_copies.append(sent)
-
-    def deviations(weight, means):
-        middle = total_of(means) * (1.0 / len(means))
-        for p, value in enumerate(means):
-            turned[p : p + 1, :] = (value - middle) * weight
+        return sent
+
+    def start_direct(j):
+        tiles = [z_tile(DIRECT[j])] * H
+        for ht, yt, piece in pieces(tiles):
+            direct[ht, yt, 2 * j] = piece
+        for ht, yt, piece in pieces([z_tile(DIRECT[j] + beside[ht]) for ht in range(H)]):
+            direct[ht, yt, 2 * j + 1] = piece
+        return exchange(direct, direct_in, sem_direct, j, pl.ds(2 * j, 2))
+
+    def start_pair(chunk):
+        first, last = PAIRED_CHUNKS[chunk]
+        for j in range(first, last):
+            for ht, yt, piece in pieces([z_tile(PAIRED[j] + beside[ht]) for ht in range(H)]):
+                pair_out[ht, j, yt] = piece
+        span = pl.ds(first, last - first)
+        return [
+            send(
+                pair_out.at[ht, span], pair_in.at[ht, span], sem_pair, (ht, chunk), z_peer(beside[ht])
+            )
+            for ht in range(H)
+        ]
+
+    direct_copies = [start_direct(0)]
+    pair_copies = [start_pair(chunk) for chunk in range(len(PAIRED_CHUNKS))]
+    direct_copies += [start_direct(j) for j in range(1, len(DIRECT))]
+    for j, e in enumerate(PAIRED):
+        for ht, yt, piece in pieces([z_tile(e)] * H):
+            paired[ht, yt, j] = piece
+
+    def fold_rows(values):
+        for p, value in enumerate(values):
+            turned[p : p + 1, :] = value
         flat = turned[...].T
-        away = []
-        for p in range(len(means)):
+        result = []
+        for p in range(len(values)):
             folded = jnp.broadcast_to(flat[0:rows, p : p + 1], (rows, LANES))
             for b in range(1, Y):
                 block = jnp.broadcast_to(flat[b * rows : (b + 1) * rows, p : p + 1], (rows, LANES))
                 folded = jnp.where(group_at == b, block, folded)
-            away.append(folded)
+            result.append(folded)
+        return result
+
+    def columns_of(means, yt):
+        kept = jnp.where(group_at == yt, means, 0.0)
+        return total_of([kept] + [pltpu.roll(kept, k * width, 1) for k in range(1, Y)])
+
+    groups = len(xy_offsets) + 1
+
+    def plane_terms(level, weight, own, others):
+        scores_of = [own[h, 16:17, :]] + [others[s, 16:17, :] for s in range(groups - 1)]
+        middle = total_of(scores_of) * (1.0 / groups)
+        away = fold_rows([(value - middle) * weight for value in scores_of])
+        means = [own[h, 0:16, :]] + [others[s, 0:16, :] for s in range(groups - 1)]
+        mean = total_of(means) * (1.0 / groups)
+        mean_xy[level] = columns_of(mean, y)
+        for p, value in enumerate(means):
+            dev_mean[level, p] = columns_of(value - mean, y)
         return middle, away
 
-    def own_columns(means):
-        kept = jnp.where(group_at == y, means, 0.0)
-        return total_of([kept] + [pltpu.roll(kept, k * width, 1) for k in range(1, Y)])
-
+    for copy in pair_aux_copies:
+        copy.wait()
+    pair_away = fold_rows(
+        [(aux[ht, 16:17, :] - aux_pair_in[ht, 16:17, :]) * (0.5 * cells) for ht in range(H)]
+    )
+    for ht in range(H):
+        aux_pair[ht, 0:17, :] = 0.5 * (aux[ht, 0:17, :] + aux_pair_in[ht, 0:17, :])
+        apart = aux[ht, 0:16, :] - aux_pair_in[ht, 0:16, :]
+        for yt in range(Y):
+            pair_dev[ht, yt] = columns_of(apart, yt)
+    aux_paired_copies = []
+    for s, (a, b) in enumerate(xy_offsets):
+        ht, yt = xy_place(a, b)
+        aux_paired_copies.append(
+            send(
+                aux_pair.at[ht],
+                aux_paired_in.at[s],
+                sem_aux_paired,
+                (s,),
+                device(z, ht, yt, xl, core),
+            )
+        )
     for copy in aux_copies:
         copy.wait()
-    groups = len(xy_offsets) + 1
-    score_xy, away = deviations(
-        float(cells), [own_mean] + [aux_in[s, 16:17, :] for s in range(groups - 1)]
-    )
-    means = [aux[h, 0:16, :]] + [aux_in[s, 0:16, :] for s in range(groups - 1)]
-    middle = total_of(means) * (1.0 / groups)
-    mean_xy[...] = own_columns(middle)
-    for p, value in enumerate(means):
-        dev_mean[p] = own_columns(value - middle)
+    score_direct, away_direct = plane_terms(0, float(cells), aux, aux_in)
+    paired_copies = []
+    for chunk, (first, last) in enumerate(PAIRED_CHUNKS):
+        for copy in pair_copies[chunk]:
+            copy.wait()
+        for j in range(first, last):
+            zt = z_tile(PAIRED[j])
+            for ht in range(H):
+                for yt in range(Y):
+                    paired[ht, yt, j] = (paired[ht, yt, j] + pair_in[ht, j, yt]) + pair_away[
+                        ht
+                    ] * pair_dev[ht, yt, pl.ds(zt, 1), :]
+        paired_copies.append(
+            exchange(paired, paired_in, sem_paired, chunk, pl.ds(first, last - first))
+        )
 
     pl.semaphore_wait(sem_far, 2)
     z_copies = []
-    for chunk in range(CHUNKS):
-        for copy in part_copies[chunk]:
+
+    def plane_sum(level, slot, own, others, i, zt, away, middle, to):
+        terms = [own[h, y, i]] + [others[s, i] for s in range(groups - 1)]
+        terms += [away[p] * dev_mean[level, p, pl.ds(zt, 1), :] for p in range(groups)]
+        zpart[slot] = total_of(terms)
+        zaux[slot, 0:1, :] = mean_xy[level, pl.ds(zt, 1), :]
+        zaux[slot, 1:2, :] = middle
+        if to is not None:
+            z_copies.append(send(zpart.at[slot], zpart_in.at[slot], sem_z, (slot,), to))
+            z_copies.append(send(zaux.at[slot], zaux_in.at[slot], sem_zaux, (slot,), to))
+
+    for j, e in enumerate(DIRECT):
+        for copy in direct_copies[j]:
             copy.wait()
-        for i in range(chunk * per_chunk, (chunk + 1) * per_chunk):
-            zt = lax.rem(z + OFFSETS[i], Z)
-            terms = [part[h, y, i]] + [part_in[s, i] for s in range(groups - 1)]
-            terms += [away[p] * dev_mean[p, pl.ds(zt, 1), :] for p in range(groups)]
-            zpart[i] = total_of(terms)
-            zaux[i, 0:1, :] = mean_xy[pl.ds(zt, 1), :]
-            zaux[i, 1:2, :] = score_xy
-            if OFFSETS[i]:
-                to = z_peer(OFFSETS[i])
-                z_copies.append(send(zpart.at[i], zpart_in.at[i], sem_z, (i,), to))
-                z_copies.append(send(zaux.at[i], zaux_in.at[i], sem_zaux, (i,), to))
+        for i, o in ((2 * j, e), (2 * j + 1, e + own_beside)):
+            plane_sum(0, i, direct, direct_in, i, z_tile(o), away_direct, score_direct, z_peer(o))
+    for copy in aux_paired_copies:
+        copy.wait()
+    score_paired, away_paired = plane_terms(1, 2.0 * cells, aux_pair, aux_paired_in)
+    alone = 2 * len(DIRECT)
+    for chunk, (first, last) in enumerate(PAIRED_CHUNKS):
+        for copy in paired_copies[chunk]:
+            copy.wait()
+        for j in range(first, last):
+            e = PAIRED[j]
+            to = z_peer(e) if e else None
+            plane_sum(
+                1, alone + j, paired, paired_in, j, z_tile(e), away_paired, score_paired, to
+            )
     for copy in z_copies:
         copy.wait()
-    _, away = deviations(
-        float(cells * groups), [zaux[Z - 1, 1:2, :]] + [zaux_in[i, 1:2, :] for i in range(Z - 1)]
-    )
-    means = [zaux[Z - 1, 0:1, :]] + [zaux_in[i, 0:1, :] for i in range(Z - 1)]
-    middle = total_of(means) * (1.0 / Z)
-    terms = [zpart[Z - 1]] + [zpart_in[i] for i in range(Z - 1)]
+    last = alone + len(PAIRED) - 1
+    shares = [1.0] * alone + [2.0] * len(PAIRED)
+    means = [zaux_in[i, 0:1, :] for i in range(last)] + [zaux[last, 0:1, :]]
+    scores_of = [zaux_in[i, 1:2, :] for i in range(last)] + [zaux[last, 1:2, :]]
+    middle = total_of([v * w for v, w in zip(scores_of, shares)]) * (1.0 / Z)
+    away = fold_rows([(v - middle) * (w * cells * groups) for v, w in zip(scores_of, shares)])
+    middle = total_of([v * w for v, w in zip(means, shares)]) * (1.0 / Z)
+    terms = [zpart[last]] + [zpart_in[i] for i in range(last)]
     terms += [far * (value - middle) for far, value in zip(away, means)]
     folded = total_of(terms)
 
@@ -330,7 +443,7 @@
         send(gram.at[plane_place(a)], gram_in.at[a - 1], sem_gram, (), plane_peer(a))
     all_of(gram.at[pl.ds(0, plane - 1)], gram_in, sem_gram)
     gram_z[...] = jnp.sum(gram_in[...], axis=0) + gram[place]
-    for a, o in enumerate(OFFSETS[: Z - 1]):
+    for a, o in enumerate(sorted(range(1, Z), key=lambda o: -min(o, Z - o))):
         send(gram_z, gram_z_in.at[a], sem_gram_z, (), z_peer(o))
     all_of(gram_z_in, gram_z_in, sem_gram_z)
     gram_all[place] = jnp.sum(gram_z_in[...], axis=0) + gram_z[...]
@@ -358,6 +471,7 @@
     cells = counts.shape[0]
     rows = comps // Y
     plane = H * XL * CORE * Y
+    tiles = 2 * len(DIRECT) + len(PAIRED)
     dma = pltpu.SemaphoreType.DMA
     hbm = pl.BlockSpec(memory_space=pltpu.HBM)
     basis_now = pl.pallas_call(
@@ -375,15 +489,23 @@
             pltpu.VMEM((H * Y - 1, 24, LANES), F32),
             pltpu.VMEM((comps + 8, LANES), F32),
             pltpu.VMEM((XL * CORE - 1, comps + 8, LANES), F32),
-            pltpu.VMEM((H, Y, Z, rows, LANES), F32),
-            pltpu.VMEM((H * Y - 1, Z, rows, LANES), F32),
-            pltpu.VMEM((H * Y, Z, LANES), F32),
-            pltpu.VMEM((Z, LANES), F32),
+            pltpu.VMEM((H, 24, LANES), F32),
+            pltpu.VMEM((H, 24, LANES), F32),
+            pltpu.VMEM((H * Y - 1, 24, LANES), F32),
+            pltpu.VMEM((H, Y, 2 * len(DIRECT), rows, LANES), F32),
+            pltpu.VMEM((H * Y - 1, 2 * len(DIRECT), rows, LANES), F32),
+            pltpu.VMEM((H, Y, len(PAIRED), rows, LANES), F32),
+            pltpu.VMEM((H * Y - 1, len(PAIRED), rows, LANES), F32),
+            pltpu.VMEM((H, len(PAIRED), Y, rows, LANES), F32),
+            pltpu.VMEM((H, len(PAIRED), Y, rows, LANES), F32),
+            pltpu.VMEM((H, Y, Z, LANES), F32),
+            pltpu.VMEM((2, H * Y, Z, LANES), F32),
+            pltpu.VMEM((2, Z, LANES), F32),
             pltpu.VMEM((LANES, LANES), F32),
-            pltpu.VMEM((Z, rows, LANES), F32),
-            pltpu.VMEM((Z, 2, LANES), F32),
-            pltpu.VMEM((Z - 1, rows, LANES), F32),
-            pltpu.VMEM((Z - 1, 2, LANES), F32),
+            pltpu.VMEM((tiles, rows, LANES), F32),
+            pltpu.VMEM((tiles, 2, LANES), F32),
+            pltpu.VMEM((tiles - 1, rows, LANES), F32),
+            pltpu.VMEM((tiles - 1, 2, LANES), F32),
             pltpu.VMEM((plane, 1, LANES), F32),
             pltpu.VMEM((plane - 1, 1, LANES), F32),
             pltpu.VMEM((1, LANES), F32),
@@ -392,9 +514,13 @@
             dma((CHUNKS + 2,)),
             dma((2, XL * CORE - 1)),
             dma((2, H * Y - 1)),
-            dma((2, H * Y - 1, CHUNKS)),
-            dma((2, Z - 1)),
-            dma((2, Z - 1)),
+            dma((2, H)),
+            dma((2, H * Y - 1)),
+            dma((2, H * Y - 1, len(DIRECT))),
+            dma((2, H, len(PAIRED_CHUNKS))),
+            dma((2, H * Y - 1, len(PAIRED_CHUNKS))),
+            dma((2, tiles - 1)),
+            dma((2, tiles - 1)),
             dma((2,)),
             dma((2,)),
             dma((2,)),

time: 59.2 us -> 57.4 us (0.970)
  Pallas kernels: 58.5 us -> 56.6 us
    pallas_call x1, Pallas kernels: 58.5 us -> 56.6 us  [on_device(): pl.pallas_call(kernel, out_shape=jax.ShapeDtypeStruct((LANES // Y, comps)...]
where the time goes in v3:
time: 57.4 us; the launch traced here: 57.3 us
  Pallas kernels  56.6 us (99%)
  other arithmetic  0.61 us (1%)
    pallas_call x1, Pallas kernels, on_device(): pl.pallas_call(kernel, out_shape=jax.ShapeDtypeStruct((LANES // Y, comps)...  56.6 us

profile of v3, /device:TPU:1, one launch (start us, length us, event | category | flops | bytes accessed | tf_op | source)
XLA Modules:
  0.0 57.3 jit_solution(12285123617662849075)
XLA Ops:
  0.0 56.6 %subspace_step.1 = f32[32,64]{1,0:T(8,128)S(1)} custom-call(bf16[128,4096]{1,0:T(8,128)(2,1)} %counts_hbm.1, s32[1,32]{1,0:T(1,128)} %occupancy_hbm.1, bf16[64,4096]{1,0:T(8,128)(2,1)} %basis_hbm.1), custom_call_target="tpu_custom_call" | custom-call | tf_op jit(solution)/shard_map/subspace_step/pallas_call | solution.py:477
  56.6 0.6 %multiply_bitcast_fusion = f32[64,32]{0,1:T(8,128)} fusion(f32[32,64]{1,0:T(8,128)S(1)} %subspace_step.1), kind=kLoop, calls=%fused_computation | loop fusion | flops 2048 | bytes 16384 | tf_op jit(solution)/shard_map/mul | solution.py:534

commit v4 on v3

--- a/solution.py
+++ b/solution.py
@@ -14,7 +14,7 @@
 LANES = 128
 DIRECT = (8, 6, 10)
 PAIRED = (4, 12, 2, 14, 0)
-PAIRED_CHUNKS = ((0, 2), (2, 5))
+PAIRED_CHUNKS = ((0, 2), (2, 4), (4, 5))
 CHUNKS = 4
 NEAR = 4
 NT = (((1,), (1,)), ((), ()))
@@ -22,6 +22,13 @@
 
 def device(z, h, y, xl, core):
     return ((z * H + h) * Y + y, xl * CORE + core)
+
+
+def far_first(offsets, weights, sizes):
+    def far(offset):
+        return -sum(w * min(o, n - o) for o, w, n in zip(offset, weights, sizes))
+
+    return sorted((o for o in offsets if any(o)), key=far)
 
 
 def total_of(values):
@@ -116,7 +123,6 @@
     sem_pair,
     sem_paired,
     sem_z,
-    sem_zaux,
     sem_gram,
     sem_gram_z,
     sem_all,
@@ -140,21 +146,28 @@
     for load in loads:
         load.start()
 
-    def send(src, dst, sems, index, to):
-        copy = pltpu.make_async_remote_copy(
+    def send(src, dst, sems, to, step=0):
+        pltpu.make_async_remote_copy(
             src_ref=src,
             dst_ref=dst,
-            send_sem=sems.at[(0, *index)],
-            recv_sem=sems.at[(1, *index)],
+            send_sem=sems.at[0, step],
+            recv_sem=sems.at[1, step],
             device_id=to,
             device_id_type=MESH,
-        )
-        copy.start()
-        return copy
-
-    def gene_peer(a):
-        other = lax.rem(genes_at + a, XL * CORE)
-        return device(z, h, y, other // CORE, lax.rem(other, CORE))
+        ).start()
+
+    def wait(all_bytes, sems, step=0):
+        pltpu.make_async_remote_copy(
+            src_ref=all_bytes,
+            dst_ref=all_bytes,
+            send_sem=sems.at[0, step],
+            recv_sem=sems.at[1, step],
+            device_id=(cells_at, genes_at),
+            device_id_type=MESH,
+        ).wait()
+
+    def gene_peer(a, b):
+        return device(z, h, y, lax.rem(xl + a, XL), lax.rem(core + b, CORE))
 
     def xy_place(a, b):
         return lax.rem(h + a, H), lax.rem(y + b, Y)
@@ -162,17 +175,13 @@
     def z_peer(o):
         return device(lax.rem(z + o + Z, Z), h, y, xl, core)
 
-    place = ((h * XL + xl) * CORE + core) * Y + y
-
-    def plane_place(a):
-        return lax.rem(place + a, plane)
-
-    def plane_peer(a):
-        other = plane_place(a)
-        in_x = other // Y
-        return device(
-            z, in_x // (XL * CORE), lax.rem(other, Y), lax.rem(in_x // CORE, XL), lax.rem(in_x, CORE)
-        )
+    in_x = h * XL + xl
+    place = (in_x * CORE + core) * Y + y
+
+    def plane_peer(a, b, c):
+        xt = lax.rem(in_x + a, H * XL)
+        coret, yt = lax.rem(core + b, CORE), lax.rem(y + c, Y)
+        return (xt * CORE + coret) * Y + yt, device(z, xt // XL, yt, lax.rem(xt, XL), coret)
 
     def z_tile(o):
         return lax.rem(z + o + Z, Z)
@@ -180,11 +189,18 @@
     beside = [1 - 2 * lax.rem(z + ht, 2) for ht in range(H)]
     own_beside = 1 - 2 * lax.rem(z + h, 2)
 
-    xy_offsets = [(a, b) for a in range(H) for b in range(Y) if a or b]
+    gene_offsets = [(1, 0), (1, 1), (0, 1)]
+    xy_offsets = far_first([(a, b) for a in range(H) for b in range(Y)], (4, 2), (H, Y))
+    plane_offsets = far_first(
+        [(a, b, c) for a in range(H * XL) for b in range(CORE) for c in range(Y)],
+        (2, 1, 2),
+        (H * XL, CORE, Y),
+    )
+    z_offsets = far_first([(o,) for o in range(Z)], (1,), (Z,))
 
     barrier = pltpu.get_barrier_semaphore()
     near = [o for o in range(1, Z) if min(o, Z - o) <= NEAR]
-    peers = [gene_peer(a) for a in range(1, XL * CORE)]
+    peers = [gene_peer(a, b) for a, b in gene_offsets]
     peers += [device(z, *xy_place(a, b), xl, core) for a, b in xy_offsets]
     peers += [z_peer(o) for o in near]
     for peer in peers:
@@ -196,60 +212,60 @@
     aux_pair[:, 16:24, :] = jnp.zeros((H, 8, LANES), F32)
     turned[...] = jnp.zeros((LANES, LANES), F32)
 
-    def center(zt, carry):
-        for ht in range(H):
-            at = pl.multiple_of((zt * H + ht) * LANES, LANES)
-            entries = counts[:, pl.ds(at, LANES)].astype(F32)
-            stored = occupancy[0, zt * H + ht].astype(F32)
-            logged = jnp.log(1.0 + entries) * stored
-            mean = jnp.sum(logged, axis=0, keepdims=True) * (1.0 / cells)
-            cbuf[:, pl.ds(at, LANES)] = (logged - mean).astype(BF16)
-            aux[ht, pl.ds(zt, 1), :] = mean
-            high = mean.astype(BF16).astype(F32)
-            middle = (mean - high).astype(BF16).astype(F32)
-            low = mean - high - middle
-            stacked = jnp.where(
-                row_at == 0, high, jnp.where(row_at == 1, middle, jnp.where(row_at == 2, low, 0.0))
-            )
-            split_mean[:, pl.ds(at, LANES)] = stacked.astype(BF16)
-        return carry
-
-    per_chunk = Z // CHUNKS
+    def center(j):
+        at = pl.ds(j * LANES, LANES)
+        entries = counts[:, at].astype(F32)
+        logged = jnp.log(1.0 + entries) * occupancy[0, j].astype(F32)
+        mean = jnp.sum(logged, axis=0, keepdims=True) * (1.0 / cells)
+        cbuf[:, at] = (logged - mean).astype(BF16)
+        aux[j % H, j // H : j // H + 1, :] = mean
+        high = mean.astype(BF16).astype(F32)
+        middle = (mean - high).astype(BF16).astype(F32)
+        low = mean - high - middle
+        stacked = jnp.where(
+            row_at == 0, high, jnp.where(row_at == 1, middle, jnp.where(row_at == 2, low, 0.0))
+        )
+        split_mean[:, at] = stacked.astype(BF16)
+
+    def product_of(c):
+        span = pl.ds(c * wide, wide)
+        return (
+            lax.dot_general(basis[:, span], cbuf[:, span], NT, preferred_element_type=F32),
+            lax.dot_general(split_mean[:, span], basis[:, span], NT, preferred_element_type=F32),
+        )
+
     loads[0].wait()
+    products = []
     for c in range(CHUNKS):
         loads[c + 1].wait()
-        lax.fori_loop(c * per_chunk, (c + 1) * per_chunk, center, 0)
-    loads[-1].wait()
-
-    score[0:comps, :] = lax.dot_general(basis[...], cbuf[...], NT, preferred_element_type=F32)
-    of_mean = lax.dot_general(split_mean[...], basis[...], NT, preferred_element_type=F32)
+        if c == 1:
+            loads[-1].wait()
+        if c:
+            products.append(product_of(c - 1))
+        for j in range(c * wide // LANES, (c + 1) * wide // LANES):
+            center(j)
+    products.append(product_of(CHUNKS - 1))
+    score[0:comps, :] = total_of([p for p, _ in products])
+    of_mean = total_of([p for _, p in products])
     score[comps : comps + 8, :] = jnp.zeros((8, LANES), F32)
     score[comps : comps + 1, 0:comps] = of_mean[0:1] + of_mean[1:2] + of_mean[2:3]
 
     pl.semaphore_wait(barrier, len(peers))
     for o in (NEAR, Z - NEAR):
         pl.semaphore_signal(sem_far, inc=1, device_id=z_peer(o), device_id_type=MESH)
-    copies = [
-        send(score, score_in.at[a - 1], sem_score, (a - 1,), gene_peer(a))
-        for a in range(1, XL * CORE)
-    ]
-    for copy in copies:
-        copy.wait()
+    for s, (a, b) in enumerate(gene_offsets):
+        send(score, score_in.at[s], sem_score, gene_peer(a, b))
+    wait(score_in, sem_score)
     whole = total_of([score[...]] + [score_in[a] for a in range(XL * CORE - 1)])
     scores, own_mean = whole[0:comps], whole[comps : comps + 1]
     for ht in range(H):
         aux[ht, 16:17, :] = own_mean
 
-    aux_copies = []
     for s, (a, b) in enumerate(xy_offsets):
         ht, yt = xy_place(a, b)
-        aux_copies.append(
-            send(aux.at[ht], aux_in.at[s], sem_aux, (s,), device(z, ht, yt, xl, core))
-        )
-
-    pair_aux_copies = [
-        send(aux.at[ht], aux_pair_in.at[ht], sem_aux_pair, (ht,), z_peer(beside[ht])) for ht in range(H)
-    ]
+        send(aux.at[ht], aux_in.at[s], sem_aux, device(z, ht, yt, xl, core))
+    for ht in range(H):
+        send(aux.at[ht], aux_pair_in.at[ht], sem_aux_pair, z_peer(beside[ht]))
 
     score_high = scores.astype(BF16)
     score_low = (scores - score_high.astype(F32)).astype(BF16)
@@ -275,19 +291,9 @@
         return result
 
     def exchange(src, dst, sems, chunk, span):
-        sent = []
         for s, (a, b) in enumerate(xy_offsets):
             ht, yt = xy_place(a, b)
-            sent.append(
-                send(
-                    src.at[ht, yt, span],
-                    dst.at[s, span],
-                    sems,
-                    (s, chunk),
-                    device(z, ht, yt, xl, core),
-                )
-            )
-        return sent
+            send(src.at[ht, yt, span], dst.at[span, s], sems, device(z, ht, yt, xl, core), chunk)
 
     def start_direct(j):
         tiles = [z_tile(DIRECT[j])] * H
@@ -295,7 +301,7 @@
             direct[ht, yt, 2 * j] = piece
         for ht, yt, piece in pieces([z_tile(DIRECT[j] + beside[ht]) for ht in range(H)]):
             direct[ht, yt, 2 * j + 1] = piece
-        return exchange(direct, direct_in, sem_direct, j, pl.ds(2 * j, 2))
+        exchange(direct, direct_in, sem_direct, j, pl.ds(2 * j, 2))
 
     def start_pair(chunk):
         first, last = PAIRED_CHUNKS[chunk]
@@ -303,16 +309,14 @@
             for ht, yt, piece in pieces([z_tile(PAIRED[j] + beside[ht]) for ht in range(H)]):
                 pair_out[ht, j, yt] = piece
         span = pl.ds(first, last - first)
-        return [
-            send(
-                pair_out.at[ht, span], pair_in.at[ht, span], sem_pair, (ht, chunk), z_peer(beside[ht])
-            )
-            for ht in range(H)
-        ]
-
-    direct_copies = [start_direct(0)]
-    pair_copies = [start_pair(chunk) for chunk in range(len(PAIRED_CHUNKS))]
-    direct_copies += [start_direct(j) for j in range(1, len(DIRECT))]
+        for ht in range(H):
+            send(pair_out.at[ht, span], pair_in.at[ht, span], sem_pair, z_peer(beside[ht]), chunk)
+
+    start_direct(0)
+    for chunk in range(len(PAIRED_CHUNKS)):
+        start_pair(chunk)
+    for j in range(1, len(DIRECT)):
+        start_direct(j)
     for j, e in enumerate(PAIRED):
         for ht, yt, piece in pieces([z_tile(e)] * H):
             paired[ht, yt, j] = piece
@@ -347,8 +351,7 @@
             dev_mean[level, p] = columns_of(value - mean, y)
         return middle, away
 
-    for copy in pair_aux_copies:
-        copy.wait()
+    wait(aux_pair_in, sem_aux_pair)
     pair_away = fold_rows(
         [(aux[ht, 16:17, :] - aux_pair_in[ht, 16:17, :]) * (0.5 * cells) for ht in range(H)]
     )
@@ -357,25 +360,11 @@
         apart = aux[ht, 0:16, :] - aux_pair_in[ht, 0:16, :]
         for yt in range(Y):
             pair_dev[ht, yt] = columns_of(apart, yt)
-    aux_paired_copies = []
     for s, (a, b) in enumerate(xy_offsets):
         ht, yt = xy_place(a, b)
-        aux_paired_copies.append(
-            send(
-                aux_pair.at[ht],
-                aux_paired_in.at[s],
-                sem_aux_paired,
-                (s,),
-                device(z, ht, yt, xl, core),
-            )
-        )
-    for copy in aux_copies:
-        copy.wait()
-    score_direct, away_direct = plane_terms(0, float(cells), aux, aux_in)
-    paired_copies = []
+        send(aux_pair.at[ht], aux_paired_in.at[s], sem_aux_paired, device(z, ht, yt, xl, core))
     for chunk, (first, last) in enumerate(PAIRED_CHUNKS):
-        for copy in pair_copies[chunk]:
-            copy.wait()
+        wait(pair_in.at[:, pl.ds(first, last - first)], sem_pair, chunk)
         for j in range(first, last):
             zt = z_tile(PAIRED[j])
             for ht in range(H):
@@ -383,43 +372,39 @@
                     paired[ht, yt, j] = (paired[ht, yt, j] + pair_in[ht, j, yt]) + pair_away[
                         ht
                     ] * pair_dev[ht, yt, pl.ds(zt, 1), :]
-        paired_copies.append(
-            exchange(paired, paired_in, sem_paired, chunk, pl.ds(first, last - first))
-        )
-
+        exchange(paired, paired_in, sem_paired, chunk, pl.ds(first, last - first))
+
+    wait(aux_in, sem_aux)
+    score_direct, away_direct = plane_terms(0, float(cells), aux, aux_in)
     pl.semaphore_wait(sem_far, 2)
-    z_copies = []
 
     def plane_sum(level, slot, own, others, i, zt, away, middle, to):
-        terms = [own[h, y, i]] + [others[s, i] for s in range(groups - 1)]
+        terms = [own[h, y, i]] + [others[i, s] for s in range(groups - 1)]
         terms += [away[p] * dev_mean[level, p, pl.ds(zt, 1), :] for p in range(groups)]
         zpart[slot] = total_of(terms)
         zaux[slot, 0:1, :] = mean_xy[level, pl.ds(zt, 1), :]
         zaux[slot, 1:2, :] = middle
         if to is not None:
-            z_copies.append(send(zpart.at[slot], zpart_in.at[slot], sem_z, (slot,), to))
-            z_copies.append(send(zaux.at[slot], zaux_in.at[slot], sem_zaux, (slot,), to))
+            send(zpart.at[slot], zpart_in.at[slot], sem_z, to)
+            send(zaux.at[slot], zaux_in.at[slot], sem_z, to, 1)
 
     for j, e in enumerate(DIRECT):
-        for copy in direct_copies[j]:
-            copy.wait()
+        wait(direct_in.at[pl.ds(2 * j, 2)], sem_direct, j)
         for i, o in ((2 * j, e), (2 * j + 1, e + own_beside)):
             plane_sum(0, i, direct, direct_in, i, z_tile(o), away_direct, score_direct, z_peer(o))
-    for copy in aux_paired_copies:
-        copy.wait()
+    wait(aux_paired_in, sem_aux_paired)
     score_paired, away_paired = plane_terms(1, 2.0 * cells, aux_pair, aux_paired_in)
     alone = 2 * len(DIRECT)
     for chunk, (first, last) in enumerate(PAIRED_CHUNKS):
-        for copy in paired_copies[chunk]:
-            copy.wait()
+        wait(paired_in.at[pl.ds(first, last - first)], sem_paired, chunk)
         for j in range(first, last):
             e = PAIRED[j]
             to = z_peer(e) if e else None
             plane_sum(
                 1, alone + j, paired, paired_in, j, z_tile(e), away_paired, score_paired, to
             )
-    for copy in z_copies:
-        copy.wait()
+    wait(zpart_in, sem_z)
+    wait(zaux_in, sem_z, 1)
     last = alone + len(PAIRED) - 1
     shares = [1.0] * alone + [2.0] * len(PAIRED)
     means = [zaux_in[i, 0:1, :] for i in range(last)] + [zaux[last, 0:1, :]]
@@ -439,31 +424,21 @@
     packed = jnp.concatenate([own_gram[0:plane], own_gram[plane:]], axis=1)
     for e in range(plane):
         gram[e] = packed[e : e + 1]
-    for a in range(1, plane):
-        send(gram.at[plane_place(a)], gram_in.at[a - 1], sem_gram, (), plane_peer(a))
-    all_of(gram.at[pl.ds(0, plane - 1)], gram_in, sem_gram)
+    for s, offset in enumerate(plane_offsets):
+        at, to = plane_peer(*offset)
+        send(gram.at[at], gram_in.at[s], sem_gram, to)
+    wait(gram_in, sem_gram)
     gram_z[...] = jnp.sum(gram_in[...], axis=0) + gram[place]
-    for a, o in enumerate(sorted(range(1, Z), key=lambda o: -min(o, Z - o))):
-        send(gram_z, gram_z_in.at[a], sem_gram_z, (), z_peer(o))
-    all_of(gram_z_in, gram_z_in, sem_gram_z)
+    for s, (o,) in enumerate(z_offsets):
+        send(gram_z, gram_z_in.at[s], sem_gram_z, z_peer(o))
+    wait(gram_z_in, sem_gram_z)
     gram_all[place] = jnp.sum(gram_z_in[...], axis=0) + gram_z[...]
-    for a in range(1, plane):
-        send(gram_all.at[place], gram_all.at[place], sem_all, (), plane_peer(a))
-    all_of(gram_all.at[pl.ds(0, plane - 1)], gram_all.at[pl.ds(0, plane - 1)], sem_all)
+    for offset in plane_offsets:
+        send(gram_all.at[place], gram_all.at[place], sem_all, plane_peer(*offset)[1])
+    wait(gram_all.at[pl.ds(0, plane - 1)], sem_all)
     packed = gram_all[...].reshape(plane, LANES)
     gram_sum = jnp.concatenate([packed[:, 0:comps], packed[:, comps : 2 * comps]], axis=0)
     out[...] = solve(gram_sum, spread).T[0:width]
-
-
-def all_of(sent, received, sems):
-    pltpu.make_async_remote_copy(
-        src_ref=sent,
-        dst_ref=received,
-        send_sem=sems.at[0],
-        recv_sem=sems.at[1],
-        device_id=(0, 0),
-        device_id_type=MESH,
-    ).wait()
 
 
 def on_device(counts, occupancy, start_basis):
@@ -493,9 +468,9 @@
             pltpu.VMEM((H, 24, LANES), F32),
             pltpu.VMEM((H * Y - 1, 24, LANES), F32),
             pltpu.VMEM((H, Y, 2 * len(DIRECT), rows, LANES), F32),
-            pltpu.VMEM((H * Y - 1, 2 * len(DIRECT), rows, LANES), F32),
+            pltpu.VMEM((2 * len(DIRECT), H * Y - 1, rows, LANES), F32),
             pltpu.VMEM((H, Y, len(PAIRED), rows, LANES), F32),
-            pltpu.VMEM((H * Y - 1, len(PAIRED), rows, LANES), F32),
+            pltpu.VMEM((len(PAIRED), H * Y - 1, rows, LANES), F32),
             pltpu.VMEM((H, len(PAIRED), Y, rows, LANES), F32),
             pltpu.VMEM((H, len(PAIRED), Y, rows, LANES), F32),
             pltpu.VMEM((H, Y, Z, LANES), F32),
@@ -512,18 +487,17 @@
             pltpu.VMEM((Z - 1, 1, LANES), F32),
             pltpu.VMEM((plane, 1, LANES), F32),
             dma((CHUNKS + 2,)),
-            dma((2, XL * CORE - 1)),
-            dma((2, H * Y - 1)),
-            dma((2, H)),
-            dma((2, H * Y - 1)),
-            dma((2, H * Y - 1, len(DIRECT))),
-            dma((2, H, len(PAIRED_CHUNKS))),
-            dma((2, H * Y - 1, len(PAIRED_CHUNKS))),
-            dma((2, tiles - 1)),
-            dma((2, tiles - 1)),
-            dma((2,)),
-            dma((2,)),
-            dma((2,)),
+            dma((2, 1)),
+            dma((2, 1)),
+            dma((2, 1)),
+            dma((2, 1)),
+            dma((2, len(DIRECT))),
+            dma((2, len(PAIRED_CHUNKS))),
+            dma((2, len(PAIRED_CHUNKS))),
+            dma((2, 2)),
+            dma((2, 1)),
+            dma((2, 1)),
+            dma((2, 1)),
             pltpu.SemaphoreType.REGULAR,
         ],
         compiler_params=pltpu.CompilerParams(

time: 57.4 us -> 55.1 us (0.960)
  Pallas kernels: 56.6 us -> 54.4 us
    pallas_call x1, Pallas kernels: 56.6 us -> 54.4 us  [on_device(): pl.pallas_call(kernel, out_shape=jax.ShapeDtypeStruct((LANES // Y, comps)...]
where the time goes in v4:
time: 55.1 us; the launch traced here: 55 us
  Pallas kernels  54.4 us (99%)
  other arithmetic  0.61 us (1%)
    pallas_call x1, Pallas kernels, on_device(): pl.pallas_call(kernel, out_shape=jax.ShapeDtypeStruct((LANES // Y, comps)...  54.4 us

profile of v4, /device:TPU:1, one launch (start us, length us, event | category | flops | bytes accessed | tf_op | source)
XLA Modules:
  0.0 55.0 jit_solution(1273106490983785510)
XLA Ops:
  0.0 54.4 %subspace_step.1 = f32[32,64]{1,0:T(8,128)S(1)} custom-call(bf16[128,4096]{1,0:T(8,128)(2,1)} %counts_hbm.1, s32[1,32]{1,0:T(1,128)} %occupancy_hbm.1, bf16[64,4096]{1,0:T(8,128)(2,1)} %basis_hbm.1), custom_call_target="tpu_custom_call" | custom-call | tf_op jit(solution)/shard_map/subspace_step/pallas_call | solution.py:452
  54.4 0.6 %multiply_bitcast_fusion = f32[64,32]{0,1:T(8,128)} fusion(f32[32,64]{1,0:T(8,128)S(1)} %subspace_step.1), kind=kLoop, calls=%fused_computation | loop fusion | flops 2048 | bytes 16384 | tf_op jit(solution)/shard_map/mul | solution.py:508

commit v5 on v4

--- a/solution.py
+++ b/solution.py
@@ -12,9 +12,9 @@
 MESH = pl.DeviceIdType.MESH
 Z, H, Y, XL, CORE = 16, 2, 4, 2, 2
 LANES = 128
-DIRECT = (8, 6, 10)
-PAIRED = (4, 12, 2, 14, 0)
-PAIRED_CHUNKS = ((0, 2), (2, 4), (4, 5))
+DIRECT = (8, 10)
+PAIRED = (6, 4, 12, 2, 14, 0)
+SCORE_ROW = 7
 CHUNKS = 4
 NEAR = 4
 NT = (((1,), (1,)), ((), ()))
@@ -88,13 +88,15 @@
     basis,
     cbuf,
     split_mean,
-    aux,
-    aux_in,
+    mean_all,
+    means_direct,
+    means_direct_in,
+    means_out,
+    means_out_in,
+    means_paired,
+    means_paired_in,
     score,
     score_in,
-    aux_pair,
-    aux_pair_in,
-    aux_paired_in,
     direct,
     direct_in,
     paired,
@@ -116,9 +118,9 @@
     gram_all,
     sem_in,
     sem_score,
-    sem_aux,
-    sem_aux_pair,
-    sem_aux_paired,
+    sem_means,
+    sem_means_out,
+    sem_means_paired,
     sem_direct,
     sem_pair,
     sem_paired,
@@ -208,8 +210,8 @@
 
     row_at = lax.broadcasted_iota(jnp.int32, (16, LANES), 0)
     group_at = lax.broadcasted_iota(jnp.int32, (16, LANES), 1) // width
-    aux[:, 16:24, :] = jnp.zeros((H, 8, LANES), F32)
-    aux_pair[:, 16:24, :] = jnp.zeros((H, 8, LANES), F32)
+    for ref in (means_direct, means_out, means_paired):
+        ref[...] = jnp.zeros(ref.shape, F32)
     turned[...] = jnp.zeros((LANES, LANES), F32)
 
     def center(j):
@@ -218,7 +220,7 @@
         logged = jnp.log(1.0 + entries) * occupancy[0, j].astype(F32)
         mean = jnp.sum(logged, axis=0, keepdims=True) * (1.0 / cells)
         cbuf[:, at] = (logged - mean).astype(BF16)
-        aux[j % H, j // H : j // H + 1, :] = mean
+        mean_all[j % H, j // H : j // H + 1, :] = mean
         high = mean.astype(BF16).astype(F32)
         middle = (mean - high).astype(BF16).astype(F32)
         low = mean - high - middle
@@ -253,20 +255,19 @@
     pl.semaphore_wait(barrier, len(peers))
     for o in (NEAR, Z - NEAR):
         pl.semaphore_signal(sem_far, inc=1, device_id=z_peer(o), device_id_type=MESH)
-    for s, (a, b) in enumerate(gene_offsets):
-        send(score, score_in.at[s], sem_score, gene_peer(a, b))
-    wait(score_in, sem_score)
-    whole = total_of([score[...]] + [score_in[a] for a in range(XL * CORE - 1)])
-    scores, own_mean = whole[0:comps], whole[comps : comps + 1]
+    of_cells, of_means = pl.ds(0, comps), pl.ds(comps, 8)
+    for step, span in enumerate((of_cells, of_means)):
+        for s, (a, b) in enumerate(gene_offsets):
+            send(score.at[span], score_in.at[s, span], sem_score, gene_peer(a, b), step)
     for ht in range(H):
-        aux[ht, 16:17, :] = own_mean
-
-    for s, (a, b) in enumerate(xy_offsets):
-        ht, yt = xy_place(a, b)
-        send(aux.at[ht], aux_in.at[s], sem_aux, device(z, ht, yt, xl, core))
-    for ht in range(H):
-        send(aux.at[ht], aux_pair_in.at[ht], sem_aux_pair, z_peer(beside[ht]))
-
+        for i in range(2 * len(DIRECT)):
+            at = z_tile(DIRECT[i // 2] + i % 2 * beside[ht])
+            means_direct[ht, i : i + 1, :] = mean_all[ht, pl.ds(at, 1), :]
+        for j, e in enumerate(PAIRED):
+            means_out[ht, j : j + 1, :] = mean_all[ht, pl.ds(z_tile(e + beside[ht]), 1), :]
+            means_paired[ht, j : j + 1, :] = mean_all[ht, pl.ds(z_tile(e), 1), :]
+    wait(score_in.at[:, of_cells], sem_score)
+    scores = total_of([score[0:comps]] + [score_in[a, 0:comps] for a in range(XL * CORE - 1)])
     score_high = scores.astype(BF16)
     score_low = (scores - score_high.astype(F32)).astype(BF16)
     stacked = jnp.concatenate([score_high, score_low], axis=0)
@@ -303,20 +304,33 @@
             direct[ht, yt, 2 * j + 1] = piece
         exchange(direct, direct_in, sem_direct, j, pl.ds(2 * j, 2))
 
-    def start_pair(chunk):
-        first, last = PAIRED_CHUNKS[chunk]
-        for j in range(first, last):
-            for ht, yt, piece in pieces([z_tile(PAIRED[j] + beside[ht]) for ht in range(H)]):
-                pair_out[ht, j, yt] = piece
-        span = pl.ds(first, last - first)
+    def start_pair(j):
+        for ht, yt, piece in pieces([z_tile(PAIRED[j] + beside[ht]) for ht in range(H)]):
+            pair_out[ht, j, yt] = piece
         for ht in range(H):
-            send(pair_out.at[ht, span], pair_in.at[ht, span], sem_pair, z_peer(beside[ht]), chunk)
-
+            send(pair_out.at[ht, j], pair_in.at[ht, j], sem_pair, z_peer(beside[ht]), j)
+
+    def send_means():
+        wait(score_in.at[:, of_means], sem_score, 1)
+        whole = total_of(
+            [score[comps : comps + 1]]
+            + [score_in[a, comps : comps + 1] for a in range(XL * CORE - 1)]
+        )
+        for ht in range(H):
+            for ref in (means_direct, means_out, means_paired):
+                ref[ht, SCORE_ROW : SCORE_ROW + 1, :] = whole
+            send(means_out.at[ht], means_out_in.at[ht], sem_means_out, z_peer(beside[ht]))
+        for s, (a, b) in enumerate(xy_offsets):
+            ht, yt = xy_place(a, b)
+            send(means_direct.at[ht], means_direct_in.at[s], sem_means, device(z, ht, yt, xl, core))
+
+    start_pair(0)
+    send_means()
     start_direct(0)
-    for chunk in range(len(PAIRED_CHUNKS)):
-        start_pair(chunk)
-    for j in range(1, len(DIRECT)):
-        start_direct(j)
+    start_pair(1)
+    start_direct(1)
+    for j in range(2, len(PAIRED)):
+        start_pair(j)
     for j, e in enumerate(PAIRED):
         for ht, yt, piece in pieces([z_tile(e)] * H):
             paired[ht, yt, j] = piece
@@ -335,74 +349,75 @@
         return result
 
     def columns_of(means, yt):
-        kept = jnp.where(group_at == yt, means, 0.0)
+        kept = jnp.where(group_at[0:8] == yt, means, 0.0)
         return total_of([kept] + [pltpu.roll(kept, k * width, 1) for k in range(1, Y)])
 
     groups = len(xy_offsets) + 1
 
     def plane_terms(level, weight, own, others):
-        scores_of = [own[h, 16:17, :]] + [others[s, 16:17, :] for s in range(groups - 1)]
-        middle = total_of(scores_of) * (1.0 / groups)
-        away = fold_rows([(value - middle) * weight for value in scores_of])
-        means = [own[h, 0:16, :]] + [others[s, 0:16, :] for s in range(groups - 1)]
-        mean = total_of(means) * (1.0 / groups)
-        mean_xy[level] = columns_of(mean, y)
-        for p, value in enumerate(means):
-            dev_mean[level, p] = columns_of(value - mean, y)
-        return middle, away
-
-    wait(aux_pair_in, sem_aux_pair)
-    pair_away = fold_rows(
-        [(aux[ht, 16:17, :] - aux_pair_in[ht, 16:17, :]) * (0.5 * cells) for ht in range(H)]
-    )
+        values = [own[h]] + [others[s] for s in range(groups - 1)]
+        middle = total_of(values) * (1.0 / groups)
+        apart = [value - middle for value in values]
+        away = fold_rows([a[SCORE_ROW : SCORE_ROW + 1] * weight for a in apart])
+        mean_xy[level] = columns_of(middle, y)
+        for p, value in enumerate(apart):
+            dev_mean[level, p] = columns_of(value, y)
+        return middle[SCORE_ROW : SCORE_ROW + 1], away
+
+    wait(means_out_in, sem_means_out)
+    apart = [means_paired[ht] - means_out_in[ht] for ht in range(H)]
+    pair_away = fold_rows([a[SCORE_ROW : SCORE_ROW + 1] * (0.5 * cells) for a in apart])
     for ht in range(H):
-        aux_pair[ht, 0:17, :] = 0.5 * (aux[ht, 0:17, :] + aux_pair_in[ht, 0:17, :])
-        apart = aux[ht, 0:16, :] - aux_pair_in[ht, 0:16, :]
+        means_paired[ht] = 0.5 * (means_paired[ht] + means_out_in[ht])
         for yt in range(Y):
-            pair_dev[ht, yt] = columns_of(apart, yt)
+            pair_dev[ht, yt] = columns_of(apart[ht], yt)
     for s, (a, b) in enumerate(xy_offsets):
         ht, yt = xy_place(a, b)
-        send(aux_pair.at[ht], aux_paired_in.at[s], sem_aux_paired, device(z, ht, yt, xl, core))
-    for chunk, (first, last) in enumerate(PAIRED_CHUNKS):
-        wait(pair_in.at[:, pl.ds(first, last - first)], sem_pair, chunk)
-        for j in range(first, last):
-            zt = z_tile(PAIRED[j])
-            for ht in range(H):
-                for yt in range(Y):
-                    paired[ht, yt, j] = (paired[ht, yt, j] + pair_in[ht, j, yt]) + pair_away[
-                        ht
-                    ] * pair_dev[ht, yt, pl.ds(zt, 1), :]
-        exchange(paired, paired_in, sem_paired, chunk, pl.ds(first, last - first))
-
-    wait(aux_in, sem_aux)
-    score_direct, away_direct = plane_terms(0, float(cells), aux, aux_in)
-    pl.semaphore_wait(sem_far, 2)
-
-    def plane_sum(level, slot, own, others, i, zt, away, middle, to):
+        send(
+            means_paired.at[ht],
+            means_paired_in.at[s],
+            sem_means_paired,
+            device(z, ht, yt, xl, core),
+        )
+    def add_pair(j):
+        wait(pair_in.at[:, j], sem_pair, j)
+        for ht in range(H):
+            for yt in range(Y):
+                paired[ht, yt, j] = (paired[ht, yt, j] + pair_in[ht, j, yt]) + pair_away[
+                    ht
+                ] * pair_dev[ht, yt, j : j + 1, :]
+        exchange(paired, paired_in, sem_paired, j, pl.ds(j, 1))
+
+    def plane_sum(level, slot, own, others, i, away, middle, to):
         terms = [own[h, y, i]] + [others[i, s] for s in range(groups - 1)]
-        terms += [away[p] * dev_mean[level, p, pl.ds(zt, 1), :] for p in range(groups)]
+        terms += [away[p] * dev_mean[level, p, i : i + 1, :] for p in range(groups)]
         zpart[slot] = total_of(terms)
-        zaux[slot, 0:1, :] = mean_xy[level, pl.ds(zt, 1), :]
+        zaux[slot, 0:1, :] = mean_xy[level, i : i + 1, :]
         zaux[slot, 1:2, :] = middle
         if to is not None:
             send(zpart.at[slot], zpart_in.at[slot], sem_z, to)
             send(zaux.at[slot], zaux_in.at[slot], sem_z, to, 1)
 
-    for j, e in enumerate(DIRECT):
+    def sum_direct(j):
         wait(direct_in.at[pl.ds(2 * j, 2)], sem_direct, j)
-        for i, o in ((2 * j, e), (2 * j + 1, e + own_beside)):
-            plane_sum(0, i, direct, direct_in, i, z_tile(o), away_direct, score_direct, z_peer(o))
-    wait(aux_paired_in, sem_aux_paired)
-    score_paired, away_paired = plane_terms(1, 2.0 * cells, aux_pair, aux_paired_in)
+        for i, o in ((2 * j, DIRECT[j]), (2 * j + 1, DIRECT[j] + own_beside)):
+            plane_sum(0, i, direct, direct_in, i, away_direct, score_direct, z_peer(o))
+
+    for j in range(len(PAIRED) - 1):
+        add_pair(j)
+    wait(means_direct_in, sem_means)
+    score_direct, away_direct = plane_terms(0, float(cells), means_direct, means_direct_in)
+    pl.semaphore_wait(sem_far, 2)
+    sum_direct(0)
+    add_pair(len(PAIRED) - 1)
+    sum_direct(1)
+    wait(means_paired_in, sem_means_paired)
+    score_paired, away_paired = plane_terms(1, 2.0 * cells, means_paired, means_paired_in)
     alone = 2 * len(DIRECT)
-    for chunk, (first, last) in enumerate(PAIRED_CHUNKS):
-        wait(paired_in.at[pl.ds(first, last - first)], sem_paired, chunk)
-        for j in range(first, last):
-            e = PAIRED[j]
-            to = z_peer(e) if e else None
-            plane_sum(
-                1, alone + j, paired, paired_in, j, z_tile(e), away_paired, score_paired, to
-            )
+    for j, e in enumerate(PAIRED):
+        wait(paired_in.at[pl.ds(j, 1)], sem_paired, j)
+        to = z_peer(e) if e else None
+        plane_sum(1, alone + j, paired, paired_in, j, away_paired, score_paired, to)
     wait(zpart_in, sem_z)
     wait(zaux_in, sem_z, 1)
     last = alone + len(PAIRED) - 1
@@ -460,22 +475,24 @@
             pltpu.VMEM((comps, genes), BF16),
             pltpu.VMEM((cells, genes), BF16),
             pltpu.VMEM((16, genes), BF16),
-            pltpu.VMEM((H, 24, LANES), F32),
-            pltpu.VMEM((H * Y - 1, 24, LANES), F32),
+            pltpu.VMEM((H, Z, LANES), F32),
+            pltpu.VMEM((H, 8, LANES), F32),
+            pltpu.VMEM((H * Y - 1, 8, LANES), F32),
+            pltpu.VMEM((H, 8, LANES), F32),
+            pltpu.VMEM((H, 8, LANES), F32),
+            pltpu.VMEM((H, 8, LANES), F32),
+            pltpu.VMEM((H * Y - 1, 8, LANES), F32),
             pltpu.VMEM((comps + 8, LANES), F32),
             pltpu.VMEM((XL * CORE - 1, comps + 8, LANES), F32),
-            pltpu.VMEM((H, 24, LANES), F32),
-            pltpu.VMEM((H, 24, LANES), F32),
-            pltpu.VMEM((H * Y - 1, 24, LANES), F32),
             pltpu.VMEM((H, Y, 2 * len(DIRECT), rows, LANES), F32),
             pltpu.VMEM((2 * len(DIRECT), H * Y - 1, rows, LANES), F32),
             pltpu.VMEM((H, Y, len(PAIRED), rows, LANES), F32),
             pltpu.VMEM((len(PAIRED), H * Y - 1, rows, LANES), F32),
             pltpu.VMEM((H, len(PAIRED), Y, rows, LANES), F32),
             pltpu.VMEM((H, len(PAIRED), Y, rows, LANES), F32),
-            pltpu.VMEM((H, Y, Z, LANES), F32),
-            pltpu.VMEM((2, H * Y, Z, LANES), F32),
-            pltpu.VMEM((2, Z, LANES), F32),
+            pltpu.VMEM((H, Y, 8, LANES), F32),
+            pltpu.VMEM((2, H * Y, 8, LANES), F32),
+            pltpu.VMEM((2, 8, LANES), F32),
             pltpu.VMEM((LANES, LANES), F32),
             pltpu.VMEM((tiles, rows, LANES), F32),
             pltpu.VMEM((tiles, 2, LANES), F32),
@@ -487,13 +504,13 @@
             pltpu.VMEM((Z - 1, 1, LANES), F32),
             pltpu.VMEM((plane, 1, LANES), F32),
             dma((CHUNKS + 2,)),
-            dma((2, 1)),
+            dma((2, 2)),
             dma((2, 1)),
             dma((2, 1)),
             dma((2, 1)),
             dma((2, len(DIRECT))),
-            dma((2, len(PAIRED_CHUNKS))),
-            dma((2, len(PAIRED_CHUNKS))),
+            dma((2, len(PAIRED))),
+            dma((2, len(PAIRED))),
             dma((2, 2)),
             dma((2, 1)),
             dma((2, 1)),

time: 55.1 us -> 54 us (0.980)
  Pallas kernels: 54.4 us -> 53.2 us
    pallas_call x1, Pallas kernels: 54.4 us -> 53.2 us  [on_device(): pl.pallas_call(kernel, out_shape=jax.ShapeDtypeStruct((LANES // Y, comps)...]
where the time goes in v5:
time: 54 us; the launch traced here: 53.9 us
  Pallas kernels  53.2 us (99%)
  other arithmetic  0.61 us (1%)
    pallas_call x1, Pallas kernels, on_device(): pl.pallas_call(kernel, out_shape=jax.ShapeDtypeStruct((LANES // Y, comps)...  53.2 us

profile of v5, /device:TPU:1, one launch (start us, length us, event | category | flops | bytes accessed | tf_op | source)
XLA Modules:
  0.0 53.9 jit_solution(1658088376966795504)
XLA Ops:
  0.0 53.2 %subspace_step.1 = f32[32,64]{1,0:T(8,128)S(1)} custom-call(bf16[128,4096]{1,0:T(8,128)(2,1)} %counts_hbm.1, s32[1,32]{1,0:T(1,128)} %occupancy_hbm.1, bf16[64,4096]{1,0:T(8,128)(2,1)} %basis_hbm.1), custom_call_target="tpu_custom_call" | custom-call | tf_op jit(solution)/shard_map/subspace_step/pallas_call | solution.py:467
  53.2 0.6 %multiply_bitcast_fusion = f32[64,32]{0,1:T(8,128)} fusion(f32[32,64]{1,0:T(8,128)S(1)} %subspace_step.1), kind=kLoop, calls=%fused_computation | loop fusion | flops 2048 | bytes 16384 | tf_op jit(solution)/shard_map/mul | solution.py:525

commit v6 on v5

--- a/solution.py
+++ b/solution.py
@@ -15,6 +15,7 @@
 DIRECT = (8, 10)
 PAIRED = (6, 4, 12, 2, 14, 0)
 SCORE_ROW = 7
+LEAD = 1
 CHUNKS = 4
 NEAR = 4
 NT = (((1,), (1,)), ((), ()))
@@ -154,19 +155,29 @@
             dst_ref=dst,
             send_sem=sems.at[0, step],
             recv_sem=sems.at[1, step],
-            device_id=to,
+            device_id=to if len(to) == 2 else device(*to),
             device_id_type=MESH,
         ).start()
 
-    def wait(all_bytes, sems, step=0):
-        pltpu.make_async_remote_copy(
+    def waiting(all_bytes, sems, step):
+        return pltpu.make_async_remote_copy(
             src_ref=all_bytes,
             dst_ref=all_bytes,
             send_sem=sems.at[0, step],
             recv_sem=sems.at[1, step],
             device_id=(cells_at, genes_at),
             device_id_type=MESH,
-        ).wait()
+        )
+
+    def wait_out(all_bytes, sems, step=0):
+        waiting(all_bytes, sems, step).wait_send()
+
+    def wait_in(all_bytes, sems, step=0):
+        waiting(all_bytes, sems, step).wait_recv()
+
+    def wait(all_bytes, sems, step=0):
+        wait_out(all_bytes, sems, step)
+        wait_in(all_bytes, sems, step)
 
     def gene_peer(a, b):
         return device(z, h, y, lax.rem(xl + a, XL), lax.rem(core + b, CORE))
@@ -178,12 +189,11 @@
         return device(lax.rem(z + o + Z, Z), h, y, xl, core)
 
     in_x = h * XL + xl
-    place = (in_x * CORE + core) * Y + y
-
-    def plane_peer(a, b, c):
-        xt = lax.rem(in_x + a, H * XL)
-        coret, yt = lax.rem(core + b, CORE), lax.rem(y + c, Y)
-        return (xt * CORE + coret) * Y + yt, device(z, xt // XL, yt, lax.rem(xt, XL), coret)
+    chip = in_x * Y + y
+
+    def chip_peer(a, c):
+        xt, yt = lax.rem(in_x + a, H * XL), lax.rem(y + c, Y)
+        return xt * Y + yt, (z, xt // XL, yt, lax.rem(xt, XL))
 
     def z_tile(o):
         return lax.rem(z + o + Z, Z)
@@ -193,11 +203,7 @@
 
     gene_offsets = [(1, 0), (1, 1), (0, 1)]
     xy_offsets = far_first([(a, b) for a in range(H) for b in range(Y)], (4, 2), (H, Y))
-    plane_offsets = far_first(
-        [(a, b, c) for a in range(H * XL) for b in range(CORE) for c in range(Y)],
-        (2, 1, 2),
-        (H * XL, CORE, Y),
-    )
+    chip_offsets = far_first([(a, c) for a in range(H * XL) for c in range(Y)], (1, 1), (H * XL, Y))
     z_offsets = far_first([(o,) for o in range(Z)], (1,), (Z,))
 
     barrier = pltpu.get_barrier_semaphore()
@@ -221,20 +227,10 @@
         mean = jnp.sum(logged, axis=0, keepdims=True) * (1.0 / cells)
         cbuf[:, at] = (logged - mean).astype(BF16)
         mean_all[j % H, j // H : j // H + 1, :] = mean
-        high = mean.astype(BF16).astype(F32)
-        middle = (mean - high).astype(BF16).astype(F32)
-        low = mean - high - middle
-        stacked = jnp.where(
-            row_at == 0, high, jnp.where(row_at == 1, middle, jnp.where(row_at == 2, low, 0.0))
-        )
-        split_mean[:, at] = stacked.astype(BF16)
 
     def product_of(c):
         span = pl.ds(c * wide, wide)
-        return (
-            lax.dot_general(basis[:, span], cbuf[:, span], NT, preferred_element_type=F32),
-            lax.dot_general(split_mean[:, span], basis[:, span], NT, preferred_element_type=F32),
-        )
+        return lax.dot_general(basis[:, span], cbuf[:, span], NT, preferred_element_type=F32)
 
     loads[0].wait()
     products = []
@@ -247,18 +243,31 @@
         for j in range(c * wide // LANES, (c + 1) * wide // LANES):
             center(j)
     products.append(product_of(CHUNKS - 1))
-    score[0:comps, :] = total_of([p for p, _ in products])
-    of_mean = total_of([p for _, p in products])
-    score[comps : comps + 8, :] = jnp.zeros((8, LANES), F32)
-    score[comps : comps + 1, 0:comps] = of_mean[0:1] + of_mean[1:2] + of_mean[2:3]
+    score[0:comps, :] = total_of(products)
 
     pl.semaphore_wait(barrier, len(peers))
     for o in (NEAR, Z - NEAR):
         pl.semaphore_signal(sem_far, inc=1, device_id=z_peer(o), device_id_type=MESH)
     of_cells, of_means = pl.ds(0, comps), pl.ds(comps, 8)
-    for step, span in enumerate((of_cells, of_means)):
+
+    def send_scores(span, step):
         for s, (a, b) in enumerate(gene_offsets):
             send(score.at[span], score_in.at[s, span], sem_score, gene_peer(a, b), step)
+
+    send_scores(of_cells, 0)
+    for j in range(Z * H):
+        mean = mean_all[j % H, j // H : j // H + 1, :]
+        high = mean.astype(BF16).astype(F32)
+        middle = (mean - high).astype(BF16).astype(F32)
+        low = mean - high - middle
+        stacked = jnp.where(
+            row_at == 0, high, jnp.where(row_at == 1, middle, jnp.where(row_at == 2, low, 0.0))
+        )
+        split_mean[:, j * LANES : (j + 1) * LANES] = stacked.astype(BF16)
+    of_mean = lax.dot_general(split_mean[...], basis[...], NT, preferred_element_type=F32)
+    score[comps : comps + 8, :] = jnp.zeros((8, LANES), F32)
+    score[comps : comps + 1, 0:comps] = of_mean[0:1] + of_mean[1:2] + of_mean[2:3]
+    send_scores(of_means, 1)
     for ht in range(H):
         for i in range(2 * len(DIRECT)):
             at = z_tile(DIRECT[i // 2] + i % 2 * beside[ht])
@@ -296,13 +305,11 @@
             ht, yt = xy_place(a, b)
             send(src.at[ht, yt, span], dst.at[span, s], sems, device(z, ht, yt, xl, core), chunk)
 
-    def start_direct(j):
-        tiles = [z_tile(DIRECT[j])] * H
-        for ht, yt, piece in pieces(tiles):
-            direct[ht, yt, 2 * j] = piece
-        for ht, yt, piece in pieces([z_tile(DIRECT[j] + beside[ht]) for ht in range(H)]):
-            direct[ht, yt, 2 * j + 1] = piece
-        exchange(direct, direct_in, sem_direct, j, pl.ds(2 * j, 2))
+    def start_direct(i):
+        e = DIRECT[i // 2]
+        for ht, yt, piece in pieces([z_tile(e + i % 2 * beside[ht]) for ht in range(H)]):
+            direct[ht, yt, i] = piece
+        exchange(direct, direct_in, sem_direct, i, pl.ds(i, 1))
 
     def start_pair(j):
         for ht, yt, piece in pieces([z_tile(PAIRED[j] + beside[ht]) for ht in range(H)]):
@@ -325,10 +332,12 @@
             send(means_direct.at[ht], means_direct_in.at[s], sem_means, device(z, ht, yt, xl, core))
 
     start_pair(0)
+    start_direct(0)
     send_means()
-    start_direct(0)
     start_pair(1)
     start_direct(1)
+    for i in range(2, 2 * len(DIRECT)):
+        start_direct(i)
     for j in range(2, len(PAIRED)):
         start_pair(j)
     for j, e in enumerate(PAIRED):
@@ -398,10 +407,10 @@
             send(zpart.at[slot], zpart_in.at[slot], sem_z, to)
             send(zaux.at[slot], zaux_in.at[slot], sem_z, to, 1)
 
-    def sum_direct(j):
-        wait(direct_in.at[pl.ds(2 * j, 2)], sem_direct, j)
-        for i, o in ((2 * j, DIRECT[j]), (2 * j + 1, DIRECT[j] + own_beside)):
-            plane_sum(0, i, direct, direct_in, i, away_direct, score_direct, z_peer(o))
+    def sum_direct(i):
+        wait(direct_in.at[pl.ds(i, 1)], sem_direct, i)
+        to = z_peer(DIRECT[i // 2] + i % 2 * own_beside)
+        plane_sum(0, i, direct, direct_in, i, away_direct, score_direct, to)
 
     for j in range(len(PAIRED) - 1):
         add_pair(j)
@@ -409,8 +418,10 @@
     score_direct, away_direct = plane_terms(0, float(cells), means_direct, means_direct_in)
     pl.semaphore_wait(sem_far, 2)
     sum_direct(0)
+    sum_direct(1)
     add_pair(len(PAIRED) - 1)
-    sum_direct(1)
+    for i in range(2, 2 * len(DIRECT)):
+        sum_direct(i)
     wait(means_paired_in, sem_means_paired)
     score_paired, away_paired = plane_terms(1, 2.0 * cells, means_paired, means_paired_in)
     alone = 2 * len(DIRECT)
@@ -436,22 +447,41 @@
     own_gram = lax.dot_general(
         spread, spread, NT, precision=lax.Precision.HIGHEST, preferred_element_type=F32
     )
-    packed = jnp.concatenate([own_gram[0:plane], own_gram[plane:]], axis=1)
-    for e in range(plane):
-        gram[e] = packed[e : e + 1]
-    for s, offset in enumerate(plane_offsets):
-        at, to = plane_peer(*offset)
-        send(gram.at[at], gram_in.at[s], sem_gram, to)
-    wait(gram_in, sem_gram)
-    gram_z[...] = jnp.sum(gram_in[...], axis=0) + gram[place]
-    for s, (o,) in enumerate(z_offsets):
-        send(gram_z, gram_z_in.at[s], sem_gram_z, z_peer(o))
-    wait(gram_z_in, sem_gram_z)
-    gram_all[place] = jnp.sum(gram_z_in[...], axis=0) + gram_z[...]
-    for offset in plane_offsets:
-        send(gram_all.at[place], gram_all.at[place], sem_all, plane_peer(*offset)[1])
-    wait(gram_all.at[pl.ds(0, plane - 1)], sem_all)
-    packed = gram_all[...].reshape(plane, LANES)
+    packed = jnp.concatenate([own_gram[0 : comps // 2], own_gram[comps // 2 :]], axis=1)
+    chips = plane // CORE
+    for e in range(chips):
+        gram[e] = packed[2 * e : 2 * e + 2]
+    leads = core == LEAD
+    for s, offset in enumerate(chip_offsets):
+        at, to = chip_peer(*offset)
+        send(gram.at[at], gram_in.at[s + (CORE - 1 - core) * (chips - 1)], sem_gram, (*to, LEAD))
+
+    @pl.when(jnp.logical_not(leads))
+    def _():
+        send(gram.at[chip], gram_in.at[plane - 2], sem_gram, (*chip_peer(0, 0)[1], LEAD))
+        wait_out(gram, sem_gram)
+
+    @pl.when(leads)
+    def _():
+        wait_out(gram.at[pl.ds(0, chips - 1)], sem_gram)
+        wait_in(gram_in, sem_gram)
+        gram_z[...] = jnp.sum(gram_in[...], axis=0) + gram[chip]
+        for s, (o,) in enumerate(z_offsets):
+            send(gram_z, gram_z_in.at[s], sem_gram_z, z_peer(o))
+        wait(gram_z_in, sem_gram_z)
+        gram_all[chip] = jnp.sum(gram_z_in[...], axis=0) + gram_z[...]
+        for offset in chip_offsets:
+            for other in range(CORE):
+                send(gram_all.at[chip], gram_all.at[chip], sem_all, (*chip_peer(*offset)[1], other))
+        send(gram_all.at[chip], gram_all.at[chip], sem_all, (*chip_peer(0, 0)[1], 1 - LEAD))
+        wait_out(gram_in, sem_all)
+        wait_in(gram_all.at[pl.ds(0, chips - 1)], sem_all)
+
+    @pl.when(jnp.logical_not(leads))
+    def _():
+        wait_in(gram_all, sem_all)
+
+    packed = gram_all[...].reshape(comps // 2, LANES)
     gram_sum = jnp.concatenate([packed[:, 0:comps], packed[:, comps : 2 * comps]], axis=0)
     out[...] = solve(gram_sum, spread).T[0:width]
 
@@ -498,17 +528,17 @@
             pltpu.VMEM((tiles, 2, LANES), F32),
             pltpu.VMEM((tiles - 1, rows, LANES), F32),
             pltpu.VMEM((tiles - 1, 2, LANES), F32),
-            pltpu.VMEM((plane, 1, LANES), F32),
-            pltpu.VMEM((plane - 1, 1, LANES), F32),
-            pltpu.VMEM((1, LANES), F32),
-            pltpu.VMEM((Z - 1, 1, LANES), F32),
-            pltpu.VMEM((plane, 1, LANES), F32),
+            pltpu.VMEM((plane // CORE, 2, LANES), F32),
+            pltpu.VMEM((plane - 1, 2, LANES), F32),
+            pltpu.VMEM((2, LANES), F32),
+            pltpu.VMEM((Z - 1, 2, LANES), F32),
+            pltpu.VMEM((plane // CORE, 2, LANES), F32),
             dma((CHUNKS + 2,)),
             dma((2, 2)),
             dma((2, 1)),
             dma((2, 1)),
             dma((2, 1)),
-            dma((2, len(DIRECT))),
+            dma((2, 2 * len(DIRECT))),
             dma((2, len(PAIRED))),
             dma((2, len(PAIRED))),
             dma((2, 2)),

time: 54 us -> 52.5 us (0.972)
  Pallas kernels: 53.2 us -> 51.7 us
    pallas_call x1, Pallas kernels: 53.2 us -> 51.7 us  [on_device(): pl.pallas_call(kernel, out_shape=jax.ShapeDtypeStruct((LANES // Y, comps)...]
where the time goes in v6:
time: 52.5 us; the launch traced here: 52.4 us
  Pallas kernels  51.7 us (98%)
  other arithmetic  0.61 us (1%)
    pallas_call x1, Pallas kernels, on_device(): pl.pallas_call(kernel, out_shape=jax.ShapeDtypeStruct((LANES // Y, comps)...  51.7 us

profile of v6, /device:TPU:1, one launch (start us, length us, event | category | flops | bytes accessed | tf_op | source)
XLA Modules:
  0.0 52.4 jit_solution(12481349506798005715)
XLA Ops:
  0.0 51.7 %subspace_step.1 = f32[32,64]{1,0:T(8,128)S(1)} custom-call(bf16[128,4096]{1,0:T(8,128)(2,1)} %counts_hbm.1, s32[1,32]{1,0:T(1,128)} %occupancy_hbm.1, bf16[64,4096]{1,0:T(8,128)(2,1)} %basis_hbm.1), custom_call_target="tpu_custom_call" | custom-call | tf_op jit(solution)/shard_map/subspace_step/pallas_call | solution.py:497
  51.7 0.6 %multiply_bitcast_fusion = f32[64,32]{0,1:T(8,128)} fusion(f32[32,64]{1,0:T(8,128)S(1)} %subspace_step.1), kind=kLoop, calls=%fused_computation | loop fusion | flops 2048 | bytes 16384 | tf_op jit(solution)/shard_map/mul | solution.py:555

commit v7 on v6

--- a/solution.py
+++ b/solution.py
@@ -16,8 +16,7 @@
 PAIRED = (6, 4, 12, 2, 14, 0)
 SCORE_ROW = 7
 LEAD = 1
-CHUNKS = 4
-NEAR = 4
+LOADS = (4, 12, 12, 4)
 NT = (((1,), (1,)), ((), ()))
 
 
@@ -129,6 +128,7 @@
     sem_gram,
     sem_gram_z,
     sem_all,
+    sem_beyond,
     sem_far,
 ):
     cells_at, genes_at = lax.axis_index("cells"), lax.axis_index("genes")
@@ -141,11 +141,13 @@
     plane = H * XL * CORE * Y
 
     loads = [pltpu.make_async_copy(occupancy_hbm, occupancy, sem_in.at[0])]
-    wide = counts.shape[1] // CHUNKS
-    for c in range(CHUNKS):
-        span = pl.ds(c * wide, wide)
-        loads.append(pltpu.make_async_copy(counts_hbm.at[:, span], counts.at[:, span], sem_in.at[c + 1]))
-    loads.append(pltpu.make_async_copy(basis_hbm, basis, sem_in.at[CHUNKS + 1]))
+    tiles = [(sum(LOADS[:c]), sum(LOADS[: c + 1])) for c in range(len(LOADS))]
+    spans = [pl.ds(first * LANES, (last - first) * LANES) for first, last in tiles]
+    for c, span in enumerate(spans):
+        loads.append(
+            pltpu.make_async_copy(counts_hbm.at[:, span], counts.at[:, span], sem_in.at[c + 1])
+        )
+    loads.append(pltpu.make_async_copy(basis_hbm, basis, sem_in.at[len(LOADS) + 1]))
     for load in loads:
         load.start()
 
@@ -182,9 +184,6 @@
     def gene_peer(a, b):
         return device(z, h, y, lax.rem(xl + a, XL), lax.rem(core + b, CORE))
 
-    def xy_place(a, b):
-        return lax.rem(h + a, H), lax.rem(y + b, Y)
-
     def z_peer(o):
         return device(lax.rem(z + o + Z, Z), h, y, xl, core)
 
@@ -203,14 +202,17 @@
 
     gene_offsets = [(1, 0), (1, 1), (0, 1)]
     xy_offsets = far_first([(a, b) for a in range(H) for b in range(Y)], (4, 2), (H, Y))
+    xy_peers = []
+    for a, b in xy_offsets:
+        ht, yt = lax.rem(h + a, H), lax.rem(y + b, Y)
+        xy_peers.append((ht, yt, device(z, ht, yt, xl, core)))
     chip_offsets = far_first([(a, c) for a in range(H * XL) for c in range(Y)], (1, 1), (H * XL, Y))
     z_offsets = far_first([(o,) for o in range(Z)], (1,), (Z,))
 
     barrier = pltpu.get_barrier_semaphore()
-    near = [o for o in range(1, Z) if min(o, Z - o) <= NEAR]
-    peers = [gene_peer(a, b) for a, b in gene_offsets]
-    peers += [device(z, *xy_place(a, b), xl, core) for a, b in xy_offsets]
-    peers += [z_peer(o) for o in near]
+    beyond = [device(z, h, lax.rem(y + b, Y), xl, core) for b in range(1, Y)] + [z_peer(2), z_peer(-2)]
+    peers = [gene_peer(a, b) for a, b in gene_offsets] + beyond
+    peers += [device(z, 1 - h, y, xl, core), z_peer(1), z_peer(-1)]
     for peer in peers:
         pl.semaphore_signal(barrier, inc=1, device_id=peer, device_id_type=MESH)
 
@@ -229,25 +231,25 @@
         mean_all[j % H, j // H : j // H + 1, :] = mean
 
     def product_of(c):
-        span = pl.ds(c * wide, wide)
+        span = spans[c]
         return lax.dot_general(basis[:, span], cbuf[:, span], NT, preferred_element_type=F32)
 
     loads[0].wait()
     products = []
-    for c in range(CHUNKS):
+    for c in range(len(LOADS)):
         loads[c + 1].wait()
         if c == 1:
             loads[-1].wait()
         if c:
             products.append(product_of(c - 1))
-        for j in range(c * wide // LANES, (c + 1) * wide // LANES):
+        for j in range(*tiles[c]):
             center(j)
-    products.append(product_of(CHUNKS - 1))
+    products.append(product_of(len(LOADS) - 1))
     score[0:comps, :] = total_of(products)
 
     pl.semaphore_wait(barrier, len(peers))
-    for o in (NEAR, Z - NEAR):
-        pl.semaphore_signal(sem_far, inc=1, device_id=z_peer(o), device_id_type=MESH)
+    for peer in beyond:
+        pl.semaphore_signal(sem_beyond, inc=1, device_id=peer, device_id_type=MESH)
     of_cells, of_means = pl.ds(0, comps), pl.ds(comps, 8)
 
     def send_scores(span, step):
@@ -275,6 +277,9 @@
         for j, e in enumerate(PAIRED):
             means_out[ht, j : j + 1, :] = mean_all[ht, pl.ds(z_tile(e + beside[ht]), 1), :]
             means_paired[ht, j : j + 1, :] = mean_all[ht, pl.ds(z_tile(e), 1), :]
+    pl.semaphore_wait(sem_beyond, len(beyond))
+    for o in (4, -4):
+        pl.semaphore_signal(sem_far, inc=1, device_id=z_peer(o), device_id_type=MESH)
     wait(score_in.at[:, of_cells], sem_score)
     scores = total_of([score[0:comps]] + [score_in[a, 0:comps] for a in range(XL * CORE - 1)])
     score_high = scores.astype(BF16)
@@ -301,15 +306,15 @@
         return result
 
     def exchange(src, dst, sems, chunk, span):
-        for s, (a, b) in enumerate(xy_offsets):
-            ht, yt = xy_place(a, b)
-            send(src.at[ht, yt, span], dst.at[span, s], sems, device(z, ht, yt, xl, core), chunk)
-
-    def start_direct(i):
-        e = DIRECT[i // 2]
-        for ht, yt, piece in pieces([z_tile(e + i % 2 * beside[ht]) for ht in range(H)]):
-            direct[ht, yt, i] = piece
-        exchange(direct, direct_in, sem_direct, i, pl.ds(i, 1))
+        for s, (ht, yt, to) in enumerate(xy_peers):
+            send(src.at[ht, yt, span], dst.at[span, s], sems, to, chunk)
+
+    def start_direct(j):
+        for i in (2 * j, 2 * j + 1):
+            tiles = [z_tile(DIRECT[j] + i % 2 * beside[ht]) for ht in range(H)]
+            for ht, yt, piece in pieces(tiles):
+                direct[ht, yt, i] = piece
+        exchange(direct, direct_in, sem_direct, j, pl.ds(2 * j, 2))
 
     def start_pair(j):
         for ht, yt, piece in pieces([z_tile(PAIRED[j] + beside[ht]) for ht in range(H)]):
@@ -327,17 +332,14 @@
             for ref in (means_direct, means_out, means_paired):
                 ref[ht, SCORE_ROW : SCORE_ROW + 1, :] = whole
             send(means_out.at[ht], means_out_in.at[ht], sem_means_out, z_peer(beside[ht]))
-        for s, (a, b) in enumerate(xy_offsets):
-            ht, yt = xy_place(a, b)
-            send(means_direct.at[ht], means_direct_in.at[s], sem_means, device(z, ht, yt, xl, core))
+        for s, (ht, _, to) in enumerate(xy_peers):
+            send(means_direct.at[ht], means_direct_in.at[s], sem_means, to)
 
     start_pair(0)
+    send_means()
     start_direct(0)
-    send_means()
     start_pair(1)
     start_direct(1)
-    for i in range(2, 2 * len(DIRECT)):
-        start_direct(i)
     for j in range(2, len(PAIRED)):
         start_pair(j)
     for j, e in enumerate(PAIRED):
@@ -380,14 +382,9 @@
         means_paired[ht] = 0.5 * (means_paired[ht] + means_out_in[ht])
         for yt in range(Y):
             pair_dev[ht, yt] = columns_of(apart[ht], yt)
-    for s, (a, b) in enumerate(xy_offsets):
-        ht, yt = xy_place(a, b)
-        send(
-            means_paired.at[ht],
-            means_paired_in.at[s],
-            sem_means_paired,
-            device(z, ht, yt, xl, core),
-        )
+    for s, (ht, _, to) in enumerate(xy_peers):
+        send(means_paired.at[ht], means_paired_in.at[s], sem_means_paired, to)
+
     def add_pair(j):
         wait(pair_in.at[:, j], sem_pair, j)
         for ht in range(H):
@@ -407,10 +404,11 @@
             send(zpart.at[slot], zpart_in.at[slot], sem_z, to)
             send(zaux.at[slot], zaux_in.at[slot], sem_z, to, 1)
 
-    def sum_direct(i):
-        wait(direct_in.at[pl.ds(i, 1)], sem_direct, i)
-        to = z_peer(DIRECT[i // 2] + i % 2 * own_beside)
-        plane_sum(0, i, direct, direct_in, i, away_direct, score_direct, to)
+    def sum_direct(j):
+        wait(direct_in.at[pl.ds(2 * j, 2)], sem_direct, j)
+        for i in (2 * j, 2 * j + 1):
+            to = z_peer(DIRECT[j] + i % 2 * own_beside)
+            plane_sum(0, i, direct, direct_in, i, away_direct, score_direct, to)
 
     for j in range(len(PAIRED) - 1):
         add_pair(j)
@@ -418,10 +416,8 @@
     score_direct, away_direct = plane_terms(0, float(cells), means_direct, means_direct_in)
     pl.semaphore_wait(sem_far, 2)
     sum_direct(0)
+    add_pair(len(PAIRED) - 1)
     sum_direct(1)
-    add_pair(len(PAIRED) - 1)
-    for i in range(2, 2 * len(DIRECT)):
-        sum_direct(i)
     wait(means_paired_in, sem_means_paired)
     score_paired, away_paired = plane_terms(1, 2.0 * cells, means_paired, means_paired_in)
     alone = 2 * len(DIRECT)
@@ -533,18 +529,19 @@
             pltpu.VMEM((2, LANES), F32),
             pltpu.VMEM((Z - 1, 2, LANES), F32),
             pltpu.VMEM((plane // CORE, 2, LANES), F32),
-            dma((CHUNKS + 2,)),
+            dma((len(LOADS) + 2,)),
             dma((2, 2)),
             dma((2, 1)),
             dma((2, 1)),
             dma((2, 1)),
-            dma((2, 2 * len(DIRECT))),
+            dma((2, len(DIRECT))),
             dma((2, len(PAIRED))),
             dma((2, len(PAIRED))),
             dma((2, 2)),
             dma((2, 1)),
             dma((2, 1)),
             dma((2, 1)),
+            pltpu.SemaphoreType.REGULAR,
             pltpu.SemaphoreType.REGULAR,
         ],
         compiler_params=pltpu.CompilerParams(

time: 52.5 us -> 51.8 us (0.987)
  Pallas kernels: 51.7 us -> 51 us
    pallas_call x1, Pallas kernels: 51.7 us -> 51 us  [on_device(): pl.pallas_call(kernel, out_shape=jax.ShapeDtypeStruct((LANES // Y, comps)...]
where the time goes in v7:
time: 51.8 us; the launch traced here: 51.7 us
  Pallas kernels  51 us (98%)
  other arithmetic  0.61 us (1%)
    pallas_call x1, Pallas kernels, on_device(): pl.pallas_call(kernel, out_shape=jax.ShapeDtypeStruct((LANES // Y, comps)...  51 us

profile of v7, /device:TPU:1, one launch (start us, length us, event | category | flops | bytes accessed | tf_op | source)
XLA Modules:
  0.0 51.7 jit_solution(17186079387364433019)
XLA Ops:
  0.0 51.0 %subspace_step.1 = f32[32,64]{1,0:T(8,128)S(1)} custom-call(bf16[128,4096]{1,0:T(8,128)(2,1)} %counts_hbm.1, s32[1,32]{1,0:T(1,128)} %occupancy_hbm.1, bf16[64,4096]{1,0:T(8,128)(2,1)} %basis_hbm.1), custom_call_target="tpu_custom_call" | custom-call | tf_op jit(solution)/shard_map/subspace_step/pallas_call | solution.py:493
  51.0 0.6 %multiply_bitcast_fusion = f32[64,32]{0,1:T(8,128)} fusion(f32[32,64]{1,0:T(8,128)S(1)} %subspace_step.1), kind=kLoop, calls=%fused_computation | loop fusion | flops 2048 | bytes 16384 | tf_op jit(solution)/shard_map/mul | solution.py:552

commit v8 on v7

--- a/solution.py
+++ b/solution.py
@@ -111,6 +111,8 @@
     zaux,
     zpart_in,
     zaux_in,
+    tile,
+    spread,
     gram,
     gram_in,
     gram_z,
@@ -125,6 +127,7 @@
     sem_pair,
     sem_paired,
     sem_z,
+    sem_tile,
     sem_gram,
     sem_gram_z,
     sem_all,
@@ -213,6 +216,7 @@
     beyond = [device(z, h, lax.rem(y + b, Y), xl, core) for b in range(1, Y)] + [z_peer(2), z_peer(-2)]
     peers = [gene_peer(a, b) for a, b in gene_offsets] + beyond
     peers += [device(z, 1 - h, y, xl, core), z_peer(1), z_peer(-1)]
+    peers += [device(z_tile(o), h, y, xl, 1 - core) for o in (1, -1, 2, -2)]
     for peer in peers:
         pl.semaphore_signal(barrier, inc=1, device_id=peer, device_id_type=MESH)
 
@@ -394,20 +398,32 @@
                 ] * pair_dev[ht, yt, j : j + 1, :]
         exchange(paired, paired_in, sem_paired, j, pl.ds(j, 1))
 
+    leads = core == LEAD
+    last = 2 * len(DIRECT) + len(PAIRED) - 1
+    after_leads = (CORE - 1 - core) * last
+
+    def lead_peer(o):
+        return device(z_tile(o), h, y, xl, LEAD)
+
     def plane_sum(level, slot, own, others, i, away, middle, to):
         terms = [own[h, y, i]] + [others[i, s] for s in range(groups - 1)]
         terms += [away[p] * dev_mean[level, p, i : i + 1, :] for p in range(groups)]
         zpart[slot] = total_of(terms)
         zaux[slot, 0:1, :] = mean_xy[level, i : i + 1, :]
         zaux[slot, 1:2, :] = middle
-        if to is not None:
-            send(zpart.at[slot], zpart_in.at[slot], sem_z, to)
-            send(zaux.at[slot], zaux_in.at[slot], sem_z, to, 1)
+        def send_sum():
+            send(zpart.at[slot], zpart_in.at[slot + after_leads], sem_z, to)
+            send(zaux.at[slot], zaux_in.at[slot + after_leads], sem_z, to, 1)
+
+        if slot < last:
+            send_sum()
+        else:
+            pl.when(jnp.logical_not(leads))(send_sum)
 
     def sum_direct(j):
         wait(direct_in.at[pl.ds(2 * j, 2)], sem_direct, j)
         for i in (2 * j, 2 * j + 1):
-            to = z_peer(DIRECT[j] + i % 2 * own_beside)
+            to = lead_peer(DIRECT[j] + i % 2 * own_beside)
             plane_sum(0, i, direct, direct_in, i, away_direct, score_direct, to)
 
     for j in range(len(PAIRED) - 1):
@@ -423,45 +439,45 @@
     alone = 2 * len(DIRECT)
     for j, e in enumerate(PAIRED):
         wait(paired_in.at[pl.ds(j, 1)], sem_paired, j)
-        to = z_peer(e) if e else None
-        plane_sum(1, alone + j, paired, paired_in, j, away_paired, score_paired, to)
-    wait(zpart_in, sem_z)
-    wait(zaux_in, sem_z, 1)
-    last = alone + len(PAIRED) - 1
-    shares = [1.0] * alone + [2.0] * len(PAIRED)
-    means = [zaux_in[i, 0:1, :] for i in range(last)] + [zaux[last, 0:1, :]]
-    scores_of = [zaux_in[i, 1:2, :] for i in range(last)] + [zaux[last, 1:2, :]]
-    middle = total_of([v * w for v, w in zip(scores_of, shares)]) * (1.0 / Z)
-    away = fold_rows([(v - middle) * (w * cells * groups) for v, w in zip(scores_of, shares)])
-    middle = total_of([v * w for v, w in zip(means, shares)]) * (1.0 / Z)
-    terms = [zpart[last]] + [zpart_in[i] for i in range(last)]
-    terms += [far * (value - middle) for far, value in zip(away, means)]
-    folded = total_of(terms)
-
-    blocks = [folded] + [pltpu.roll(folded, (Y - b) * width, 1) for b in range(1, Y)]
-    spread = jnp.concatenate([jnp.where(group_at == 0, block, 0.0) for block in blocks], axis=0)
-    own_gram = lax.dot_general(
-        spread, spread, NT, precision=lax.Precision.HIGHEST, preferred_element_type=F32
-    )
-    packed = jnp.concatenate([own_gram[0 : comps // 2], own_gram[comps // 2 :]], axis=1)
+        plane_sum(1, alone + j, paired, paired_in, j, away_paired, score_paired, lead_peer(e))
+    def columns(folded, group):
+        turns = [pltpu.roll(folded, (Y - b + group) % Y * width, 1) if b != group else folded for b in range(Y)]
+        return [jnp.where(group_at == group, turn, 0.0) for turn in turns]
+
     chips = plane // CORE
-    for e in range(chips):
-        gram[e] = packed[2 * e : 2 * e + 2]
-    leads = core == LEAD
-    for s, offset in enumerate(chip_offsets):
-        at, to = chip_peer(*offset)
-        send(gram.at[at], gram_in.at[s + (CORE - 1 - core) * (chips - 1)], sem_gram, (*to, LEAD))
-
-    @pl.when(jnp.logical_not(leads))
-    def _():
-        send(gram.at[chip], gram_in.at[plane - 2], sem_gram, (*chip_peer(0, 0)[1], LEAD))
-        wait_out(gram, sem_gram)
 
     @pl.when(leads)
     def _():
+        wait_out(zpart.at[pl.ds(0, last)], sem_z)
+        wait_out(zaux.at[pl.ds(0, last)], sem_z, 1)
+        wait_in(zpart_in, sem_z)
+        wait_in(zaux_in, sem_z, 1)
+        shares = [1.0] * alone + [2.0] * len(PAIRED)
+        scores_of = [zaux_in[i, 1:2, :] for i in range(last)] + [zaux[last, 1:2, :]]
+        middle = total_of([v * w for v, w in zip(scores_of, shares)]) * (1.0 / Z)
+        away = fold_rows([(v - middle) * (w * cells * groups) for v, w in zip(scores_of, shares)])
+        own = [zpart_in[i] for i in range(last)] + [zpart[last]]
+        own_means = [zaux_in[i, 0:1, :] for i in range(last)] + [zaux[last, 0:1, :]]
+        others = [zpart_in[i] for i in range(last, 2 * last + 1)]
+        other_means = [zaux_in[i, 0:1, :] for i in range(last, 2 * last + 1)]
+        for t, (sums, means) in enumerate(((own, own_means), (others, other_means))):
+            middle = total_of([v * w for v, w in zip(means, shares)]) * (1.0 / Z)
+            tile[t] = total_of(sums + [far * (v - middle) for far, v in zip(away, means)])
+        send(tile.at[1], tile.at[0], sem_tile, (z, h, y, xl, 1 - LEAD))
+        both = [a + b for a, b in zip(columns(tile[0], 0), columns(tile[1], 1))]
+        spread[...] = jnp.concatenate(both, axis=0)
+        own_gram = lax.dot_general(
+            spread[...], spread[...], NT, precision=lax.Precision.HIGHEST, preferred_element_type=F32
+        )
+        packed = jnp.concatenate([own_gram[0 : comps // 2], own_gram[comps // 2 :]], axis=1)
+        for e in range(chips):
+            gram[e] = packed[2 * e : 2 * e + 2]
+        for s, offset in enumerate(chip_offsets):
+            at, to = chip_peer(*offset)
+            send(gram.at[at], gram_in.at[s], sem_gram, (*to, LEAD))
         wait_out(gram.at[pl.ds(0, chips - 1)], sem_gram)
-        wait_in(gram_in, sem_gram)
-        gram_z[...] = jnp.sum(gram_in[...], axis=0) + gram[chip]
+        wait_in(gram_in.at[pl.ds(0, chips - 1)], sem_gram)
+        gram_z[...] = jnp.sum(gram_in[0 : chips - 1], axis=0) + gram[chip]
         for s, (o,) in enumerate(z_offsets):
             send(gram_z, gram_z_in.at[s], sem_gram_z, z_peer(o))
         wait(gram_z_in, sem_gram_z)
@@ -470,16 +486,21 @@
             for other in range(CORE):
                 send(gram_all.at[chip], gram_all.at[chip], sem_all, (*chip_peer(*offset)[1], other))
         send(gram_all.at[chip], gram_all.at[chip], sem_all, (*chip_peer(0, 0)[1], 1 - LEAD))
+        wait_out(tile.at[1], sem_tile)
         wait_out(gram_in, sem_all)
         wait_in(gram_all.at[pl.ds(0, chips - 1)], sem_all)
 
     @pl.when(jnp.logical_not(leads))
     def _():
+        wait_out(zpart, sem_z)
+        wait_out(zaux, sem_z, 1)
+        wait_in(tile.at[0], sem_tile)
+        spread[...] = jnp.concatenate(columns(tile[0], 0), axis=0)
         wait_in(gram_all, sem_all)
 
     packed = gram_all[...].reshape(comps // 2, LANES)
     gram_sum = jnp.concatenate([packed[:, 0:comps], packed[:, comps : 2 * comps]], axis=0)
-    out[...] = solve(gram_sum, spread).T[0:width]
+    out[...] = solve(gram_sum, spread[...]).T[0:width]
 
 
 def on_device(counts, occupancy, start_basis):
@@ -522,8 +543,10 @@
             pltpu.VMEM((LANES, LANES), F32),
             pltpu.VMEM((tiles, rows, LANES), F32),
             pltpu.VMEM((tiles, 2, LANES), F32),
-            pltpu.VMEM((tiles - 1, rows, LANES), F32),
-            pltpu.VMEM((tiles - 1, 2, LANES), F32),
+            pltpu.VMEM((CORE * tiles - 1, rows, LANES), F32),
+            pltpu.VMEM((CORE * tiles - 1, 2, LANES), F32),
+            pltpu.VMEM((CORE, rows, LANES), F32),
+            pltpu.VMEM((comps, LANES), F32),
             pltpu.VMEM((plane // CORE, 2, LANES), F32),
             pltpu.VMEM((plane - 1, 2, LANES), F32),
             pltpu.VMEM((2, LANES), F32),
@@ -538,6 +561,7 @@
             dma((2, len(PAIRED))),
             dma((2, len(PAIRED))),
             dma((2, 2)),
+            dma((2, 1)),
             dma((2, 1)),
             dma((2, 1)),
             dma((2, 1)),

time: 51.8 us -> 50.9 us (0.983)
  Pallas kernels: 51 us -> 50.1 us
    pallas_call x1, Pallas kernels: 51 us -> 50.1 us  [on_device(): pl.pallas_call(kernel, out_shape=jax.ShapeDtypeStruct((LANES // Y, comps)...]
where the time goes in v8:
time: 50.9 us; the launch traced here: 50.7 us
  Pallas kernels  50.1 us (98%)
  other arithmetic  0.61 us (1%)
    pallas_call x1, Pallas kernels, on_device(): pl.pallas_call(kernel, out_shape=jax.ShapeDtypeStruct((LANES // Y, comps)...  50.1 us

profile of v8, /device:TPU:1, one launch (start us, length us, event | category | flops | bytes accessed | tf_op | source)
XLA Modules:
  0.0 50.7 jit_solution(3254478228507374255)
XLA Ops:
  0.0 50.1 %subspace_step.1 = f32[32,64]{1,0:T(8,128)S(1)} custom-call(bf16[128,4096]{1,0:T(8,128)(2,1)} %counts_hbm.1, s32[1,32]{1,0:T(1,128)} %occupancy_hbm.1, bf16[64,4096]{1,0:T(8,128)(2,1)} %basis_hbm.1), custom_call_target="tpu_custom_call" | custom-call | tf_op jit(solution)/shard_map/subspace_step/pallas_call | solution.py:514
  50.1 0.6 %multiply_bitcast_fusion = f32[64,32]{0,1:T(8,128)} fusion(f32[32,64]{1,0:T(8,128)S(1)} %subspace_step.1), kind=kLoop, calls=%fused_computation | loop fusion | flops 2048 | bytes 16384 | tf_op jit(solution)/shard_map/mul | solution.py:576

commit v9 on v8

--- a/solution.py
+++ b/solution.py
@@ -16,7 +16,7 @@
 PAIRED = (6, 4, 12, 2, 14, 0)
 SCORE_ROW = 7
 LEAD = 1
-LOADS = (4, 12, 12, 4)
+LOADS = (16, 16)
 NT = (((1,), (1,)), ((), ()))
 
 

time: 50.9 us -> 50.8 us (level)
  no operation moved by 1% of the time
where the time goes in v9:
time: 50.8 us; the launch traced here: 50.7 us
  Pallas kernels  50 us (98%)
  other arithmetic  0.61 us (1%)
    pallas_call x1, Pallas kernels, on_device(): pl.pallas_call(kernel, out_shape=jax.ShapeDtypeStruct((LANES // Y, comps)...  50 us

profile of v9, /device:TPU:1, one launch (start us, length us, event | category | flops | bytes accessed | tf_op | source)
XLA Modules:
  0.0 50.7 jit_solution(12629632951531532630)
XLA Ops:
  0.0 50.0 %subspace_step.1 = f32[32,64]{1,0:T(8,128)S(1)} custom-call(bf16[128,4096]{1,0:T(8,128)(2,1)} %counts_hbm.1, s32[1,32]{1,0:T(1,128)} %occupancy_hbm.1, bf16[64,4096]{1,0:T(8,128)(2,1)} %basis_hbm.1), custom_call_target="tpu_custom_call" | custom-call | tf_op jit(solution)/shard_map/subspace_step/pallas_call | solution.py:514
  50.1 0.6 %multiply_bitcast_fusion = f32[64,32]{0,1:T(8,128)} fusion(f32[32,64]{1,0:T(8,128)S(1)} %subspace_step.1), kind=kLoop, calls=%fused_computation | loop fusion | flops 2048 | bytes 16384 | tf_op jit(solution)/shard_map/mul | solution.py:576

commit v10 on v9

--- a/solution.py
+++ b/solution.py
@@ -38,21 +38,19 @@
     return values[0]
 
 
-def solve(gram, right):
-    blocks = gram.shape[0] // 8
-    left = [gram[8 * b : 8 * b + 8] for b in range(blocks)]
-    right = [right[8 * b : 8 * b + 8] for b in range(blocks)]
+def solve(joint, start):
+    blocks = joint.shape[0] // 8
+    joint = [joint[8 * b : 8 * b + 8] for b in range(blocks)]
     row_at = lax.broadcasted_iota(jnp.int32, (8, LANES), 0)
     done = []
     for kb in range(blocks):
-        cols = [
-            [
-                jnp.broadcast_to(left[b][:, 8 * kb + j : 8 * kb + j + 1], (8, LANES))
-                for j in range(8)
-            ]
-            for b in range(kb, blocks)
-        ]
-        rows_left, rows_right = left[kb], right[kb]
+        cols = []
+        for b in range(kb, blocks):
+            at = start + 8 * kb
+            cols.append(
+                [jnp.broadcast_to(joint[b][:, at + j : at + j + 1], (8, LANES)) for j in range(8)]
+            )
+        block = joint[kb]
         scale = jnp.zeros((8, LANES), F32)
         steps = []
         for j in range(8):
@@ -64,17 +62,13 @@
                 entry = jnp.broadcast_to(lower[0][m : m + 1], (8, LANES))
                 for c, low in zip(cols, lower):
                     c[m] = c[m] - low * entry
-            below = jnp.where(row_at > j, lower[0], 0.0)
-            unit_left = jnp.broadcast_to(rows_left[j : j + 1], rows_left.shape) * inv[:, : rows_left.shape[1]]
-            unit_right = jnp.broadcast_to(rows_right[j : j + 1], rows_right.shape) * inv
-            rows_left = rows_left - below[:, : rows_left.shape[1]] * unit_left
-            rows_right = rows_right - below * unit_right
-            steps.append((lower[1:], unit_left, unit_right))
-        done.append(rows_right * scale)
+            unit = jnp.broadcast_to(block[j : j + 1], (8, LANES)) * inv
+            block = block - jnp.where(row_at > j, lower[0], 0.0) * unit
+            steps.append((lower[1:], unit))
+        done.append(block * scale)
         for at, b in enumerate(range(kb + 1, blocks)):
-            for lower, unit_left, unit_right in steps:
-                left[b] = left[b] - lower[at][:, : unit_left.shape[1]] * unit_left
-                right[b] = right[b] - lower[at] * unit_right
+            for lower, unit in steps:
+                joint[b] = joint[b] - lower[at] * unit
     return jnp.concatenate(done, axis=0)
 
 
@@ -252,8 +246,6 @@
     score[0:comps, :] = total_of(products)
 
     pl.semaphore_wait(barrier, len(peers))
-    for peer in beyond:
-        pl.semaphore_signal(sem_beyond, inc=1, device_id=peer, device_id_type=MESH)
     of_cells, of_means = pl.ds(0, comps), pl.ds(comps, 8)
 
     def send_scores(span, step):
@@ -261,6 +253,8 @@
             send(score.at[span], score_in.at[s, span], sem_score, gene_peer(a, b), step)
 
     send_scores(of_cells, 0)
+    for peer in beyond:
+        pl.semaphore_signal(sem_beyond, inc=1, device_id=peer, device_id_type=MESH)
     for j in range(Z * H):
         mean = mean_all[j % H, j // H : j // H + 1, :]
         high = mean.astype(BF16).astype(F32)
@@ -498,9 +492,17 @@
         spread[...] = jnp.concatenate(columns(tile[0], 0), axis=0)
         wait_in(gram_all, sem_all)
 
-    packed = gram_all[...].reshape(comps // 2, LANES)
-    gram_sum = jnp.concatenate([packed[:, 0:comps], packed[:, comps : 2 * comps]], axis=0)
-    out[...] = solve(gram_sum, spread[...]).T[0:width]
+    half = comps // 2
+    packed = gram_all[...].reshape(half, LANES)
+    in_gram = lax.broadcasted_iota(jnp.int32, (half, LANES), 1) >= comps
+    joint = jnp.concatenate(
+        [
+            jnp.where(in_gram, pltpu.roll(packed, comps, 1), spread[0:half]),
+            jnp.where(in_gram, packed, spread[half:comps]),
+        ],
+        axis=0,
+    )
+    out[...] = solve(joint, comps).T[0:width]
 
 
 def on_device(counts, occupancy, start_basis):

time: 50.8 us -> 50.9 us (level)
  no operation moved by 1% of the time
where the time goes in v10:
time: 50.9 us; the launch traced here: 50.8 us
  Pallas kernels  50.1 us (98%)
  other arithmetic  0.61 us (1%)
    pallas_call x1, Pallas kernels, on_device(): pl.pallas_call(kernel, out_shape=jax.ShapeDtypeStruct((LANES // Y, comps)...  50.1 us

profile of v10, /device:TPU:1, one launch (start us, length us, event | category | flops | bytes accessed | tf_op | source)
XLA Modules:
  0.0 50.8 jit_solution(15693344985641252898)
XLA Ops:
  0.0 50.1 %subspace_step.1 = f32[32,64]{1,0:T(8,128)S(1)} custom-call(bf16[128,4096]{1,0:T(8,128)(2,1)} %counts_hbm.1, s32[1,32]{1,0:T(1,128)} %occupancy_hbm.1, bf16[64,4096]{1,0:T(8,128)(2,1)} %basis_hbm.1), custom_call_target="tpu_custom_call" | custom-call | tf_op jit(solution)/shard_map/subspace_step/pallas_call | solution.py:516
  50.2 0.6 %multiply_bitcast_fusion = f32[64,32]{0,1:T(8,128)} fusion(f32[32,64]{1,0:T(8,128)S(1)} %subspace_step.1), kind=kLoop, calls=%fused_computation | loop fusion | flops 2048 | bytes 16384 | tf_op jit(solution)/shard_map/mul | solution.py:578

commit v11 on v10

--- a/solution.py
+++ b/solution.py
@@ -246,6 +246,8 @@
     score[0:comps, :] = total_of(products)
 
     pl.semaphore_wait(barrier, len(peers))
+    for peer in beyond:
+        pl.semaphore_signal(sem_beyond, inc=1, device_id=peer, device_id_type=MESH)
     of_cells, of_means = pl.ds(0, comps), pl.ds(comps, 8)
 
     def send_scores(span, step):
@@ -253,8 +255,6 @@
             send(score.at[span], score_in.at[s, span], sem_score, gene_peer(a, b), step)
 
     send_scores(of_cells, 0)
-    for peer in beyond:
-        pl.semaphore_signal(sem_beyond, inc=1, device_id=peer, device_id_type=MESH)
     for j in range(Z * H):
         mean = mean_all[j % H, j // H : j // H + 1, :]
         high = mean.astype(BF16).astype(F32)

time: 50.9 us -> 50.9 us (level)
  no operation moved by 1% of the time
where the time goes in v11:
time: 50.9 us; the launch traced here: 50.8 us
  Pallas kernels  50.1 us (98%)
  other arithmetic  0.61 us (1%)
    pallas_call x1, Pallas kernels, on_device(): pl.pallas_call(kernel, out_shape=jax.ShapeDtypeStruct((LANES // Y, comps)...  50.1 us

profile of v11, /device:TPU:1, one launch (start us, length us, event | category | flops | bytes accessed | tf_op | source)
XLA Modules:
  0.0 50.8 jit_solution(2750863694838231544)
XLA Ops:
  0.0 50.1 %subspace_step.1 = f32[32,64]{1,0:T(8,128)S(1)} custom-call(bf16[128,4096]{1,0:T(8,128)(2,1)} %counts_hbm.1, s32[1,32]{1,0:T(1,128)} %occupancy_hbm.1, bf16[64,4096]{1,0:T(8,128)(2,1)} %basis_hbm.1), custom_call_target="tpu_custom_call" | custom-call | tf_op jit(solution)/shard_map/subspace_step/pallas_call | solution.py:516
  50.2 0.6 %multiply_bitcast_fusion = f32[64,32]{0,1:T(8,128)} fusion(f32[32,64]{1,0:T(8,128)S(1)} %subspace_step.1), kind=kLoop, calls=%fused_computation | loop fusion | flops 2048 | bytes 16384 | tf_op jit(solution)/shard_map/mul | solution.py:578
